TPU v7x, 512 devices: a whole 4x4x16 slice. The times are simulated.
512 devices in a mesh: pair: 16 (over y, x), side: 2 (over z_hi), blk: 16 (over z_lo, core).
Axes of the slice: x: 4, y: 4, z: 16 (z_hi: 2, z_lo: 8; z = z_hi * 8 + z_lo), core: 2. Of those that a mesh axis runs over, the one named last changes fastest.
Arguments:
- intersect: float32 [65536, 768], P(('pair', 'side', 'blk')), parts along dimension 0, may hold values from -0.1 to 1.7, as said below
- half_factors: float32 [65536, 384], P(('pair', 'side', 'blk')), parts along dimension 0, may hold values from -0.03 to 1.35, as said below
- z_pattern: int32 [512, 6], P(('pair', 'side', 'blk')), parts along dimension 0, may hold values 0 or 1
Outputs:
- refined_factor: float32 [65536, 768], P(('pair', 'side', 'blk')), parts along dimension 0
There are 16 independent parts, one for each index of `pair`. A program takes and returns all parts, laid end to end along the dimension named above; each array names one. Nothing has to cross between parts.
Inputs may be any that keep to these rules, and one draw needn't show every extreme that they name: As a whole windowed matrix, intersect is symmetric: S[a, b] = S[b, a]. `half_factors`: entries of the other half and outside the grid of blocks are absent or zero. `z_pattern`: 1 keeps a tile of the factor, 0 drops it; diagonal tiles are kept whatever it says.
All inputs are finite; a program needn't handle non-finite values. No bound on the sum of `z_pattern` on one device may be relied on, other than what follows from the above.
Results may differ from a plain program's by a relative error of at most 0.0001.
Values sent between devices are 32-bit elements; how exact they have to be, the bound alone decides.
A program may use at most 64 MiB of HBM per device.

v0:
```python
import jax
import jax.numpy as jnp
from jax import lax
from jax.sharding import PartitionSpec as P

ITERS = 2


def from_behind(shard, axis, by):
    size = lax.axis_size(axis)
    pairs = [(i, i + by) for i in range(size) if 0 <= i + by < size]
    return lax.ppermute(shard, axis, pairs)


def swapped(block, axis, stride):
    count = lax.axis_size(axis)
    route = []
    for low in range(count):
        high = low | 1 << stride
        if high != low and high < count:
            route += [(low, high), (high, low)]
    return lax.ppermute(block, axis, route)


def assemble(stack, from_lower, from_upper):
    count = stack.shape[0]
    rows = stack.shape[1]
    panels = stack.reshape(count, rows, 3, -1)
    empty = jnp.zeros_like(panels[:, :, :1])
    lower = jnp.concatenate((empty, from_lower), axis=2)
    upper = jnp.concatenate((from_upper, empty), axis=2)
    joined = jnp.stack((lower, panels, upper), axis=1)
    return joined.reshape(count, 3, rows, -1)


def pair_blocks(both):
    panels = both.reshape(both.shape[0], both.shape[1], 3, -1)
    from_lower = from_behind(panels[:, :, 1:], "blk", 1)
    from_upper = from_behind(panels[:, :, :2], "blk", -1)
    return assemble(both, from_lower, from_upper)


def neighbours(panel):
    side = lax.axis_index("side")
    other = swapped(panel, "side", 0)
    both = jnp.stack((jnp.where(side == 0, panel, other), jnp.where(side == 0, other, panel)))
    return pair_blocks(both)


def window_product(left, nearby):
    outputs = []
    for target in range(3):
        total = None
        for slot in range(3):
            source = target + 1 - slot
            if 0 <= source <= 2:
                term = lax.dot_general(
                    left[:, slot],
                    nearby[:, slot, :, source],
                    (((1, 2), (0, 1)), ((), ())),
                    precision=lax.Precision.HIGHEST,
                    preferred_element_type=jnp.float32,
                )
                total = term if total is None else total + term
        outputs.append(total)
    return jnp.stack(outputs, axis=1)


def window_cross(near_factor, near_image, side):
    mines = []
    for slot in range(3):
        column = near_factor[:, slot, :, 2 - slot]
        mines.append(lax.dynamic_index_in_dim(column, side, axis=2, keepdims=False))
    outputs = []
    for target in range(3):
        total = None
        for slot in range(3):
            source = target + 1 - slot
            if 0 <= source <= 2:
                term = lax.dot_general(
                    mines[slot],
                    near_image[:, slot, :, source],
                    (((0, 1), (0, 1)), ((), ())),
                    precision=lax.Precision.HIGHEST,
                    preferred_element_type=jnp.float32,
                )
                total = term if total is None else total + term
        outputs.append(total)
    return jnp.stack(outputs, axis=1)


def window_keep(pattern, tile, side):
    count = pattern.shape[0]
    grid = pattern.reshape(count, 3, 2, count)
    slots = jnp.arange(3)[None, :, None, None]
    halves = jnp.arange(2)[None, None, :, None]
    row_tiles = jnp.arange(count)[:, None, None, None]
    col_tiles = jnp.arange(count)[None, None, None, :]
    diagonal = ((slots == 1) & (halves == side) & (row_tiles == col_tiles)).astype(jnp.int32)
    kept = jnp.maximum(grid, diagonal).astype(jnp.float32)
    wide = jnp.broadcast_to(kept[:, None, :, :, :, None], (count, tile, 3, 2, count, tile))
    return wide.reshape(count * tile, 3, 2, count * tile)


def per_device(intersect, half_factors, z_pattern):
    rows = intersect.shape[0]
    tile = rows // z_pattern.shape[0]
    side = lax.axis_index("side")
    eye_side = jnp.eye(2, dtype=jnp.float32)
    own_side = (jnp.arange(2) == side).astype(jnp.float32)
    intersect_win = intersect.reshape(rows, 3, 2, rows)
    keep = window_keep(z_pattern, tile, side)
    slots = jnp.arange(3)[None, :, None, None]
    halves = jnp.arange(2)[None, None, :, None]
    row_ids = jnp.arange(rows)[:, None, None, None]
    col_ids = jnp.arange(rows)[None, None, None, :]
    identity = ((slots == 1) & (halves == side) & (row_ids == col_ids)).astype(jnp.float32)
    half_win = half_factors.reshape(rows, 3, rows)
    factor = half_win[:, :, None, :] * own_side[None, None, :, None]
    near_half = neighbours(half_factors).reshape(2, 3, rows, 3, rows)
    near_factor = near_half[:, :, :, :, None, :] * eye_side[:, None, None, None, :, None]
    for step in range(ITERS):
        if step > 0:
            near_factor = neighbours(factor.reshape(rows, 6 * rows)).reshape(2, 3, rows, 3, 2, rows)
        image = window_product(intersect_win, near_factor)
        near_image = neighbours(image.reshape(rows, 6 * rows)).reshape(2, 3, rows, 3, 2, rows)
        delta = identity - window_cross(near_factor, near_image, side)
        near_delta = neighbours(delta.reshape(rows, 6 * rows)).reshape(2, 3, rows, 3, 2, rows)
        first = window_product(factor, near_delta)
        second = window_product(first, near_delta)
        factor = keep * (factor + 0.5 * first + 0.375 * second)
    return factor.reshape(rows, 6 * rows)


def solution(mesh):
    return jax.shard_map(
        per_device,
        mesh=mesh,
        in_specs=(
            P(("pair", "side", "blk"), None),
            P(("pair", "side", "blk"), None),
            P(("pair", "side", "blk"), None),
        ),
        out_specs=P(("pair", "side", "blk"), None),
        check_vma=False,
    )
```

profile of v0, /device:TPU:15, one launch (start us, length us, event | category | flops | bytes accessed | tf_op | source)
XLA Modules:
  0.0 353.0 jit_solution(9689396403626887591)
XLA Ops:
  1.1 15.4 %collective-permute-start = (f32[128,384]{0,1:T(8,128)S(1)}, f32[128,384]{0,1:T(8,128)S(1)}, u32[]{:S(2)}, u32[]{:S(2)}) collective-permute-start(f32[128,384]{0,1:T(8,128)S(1)} %copy.55), channel_id=1, source_target_pairs={{0,16},{16,0},{1,17},{17,1},{2,18},{18,2},{3,19},{19,3},{4,20},{20... | collective-permute-start | bytes 589832 | tf_op jit(solution)/shard_map/ppermute | solution.py:22
  16.6 4.6 %collective-permute-done = f32[128,384]{0,1:T(8,128)S(1)} collective-permute-done((f32[128,384]{0,1:T(8,128)S(1)}, f32[128,384]{0,1:T(8,128)S(1)}, u32[]{:S(2)}, u32[]{:S(2)}) %collective-permute-start) | collective-permute-done | bytes 196640 | tf_op jit(solution)/shard_map/ppermute | solution.py:22
  21.2 3.5 collective-permute-start.2
  24.7 12.8 %collective-permute-start.1 = (f32[2,128,2,128]{1,3,2,0:T(8,128)S(1)}, f32[2,128,2,128]{1,3,2,0:T(8,128)S(1)}, u32[]{:S(2)}, u32[]{:S(2)}) collective-permute-start(f32[2,128,2,128]{1,3,2,0:T(8,128)S(1)} %get-tuple-element.53), channel_id=1, source_target_pairs={{0,1},{1,2},{2,3},{3,4},{4,5},{5,6},{6,7},{7,8},{8,9},{9,10},{10,1... | collective-permute-start | bytes 786440 | tf_op jit(solution)/shard_map/ppermute | solution.py:12
  37.7 1.9 collective-permute-done.2
  44.0 12.5 %collective-permute-start.3 = (f32[128,768]{0,1:T(8,128)S(1)}, f32[128,768]{0,1:T(8,128)}, u32[]{:S(2)}, u32[]{:S(2)}) collective-permute-start(f32[128,768]{0,1:T(8,128)S(1)} %bitcast.769), channel_id=1, source_target_pairs={{0,16},{16,0},{1,17},{17,1},{2,18},{18,2},{3,19},{19,3},{4,20},{20... | collective-permute-start | bytes 1179656 | tf_op jit(solution)/shard_map/ppermute | solution.py:22
  58.2 3.8 %collective-permute-done.3 = f32[128,768]{0,1:T(8,128)} collective-permute-done((f32[128,768]{0,1:T(8,128)S(1)}, f32[128,768]{0,1:T(8,128)}, u32[]{:S(2)}, u32[]{:S(2)}) %collective-permute-start.3) | collective-permute-done | bytes 393248 | tf_op jit(solution)/shard_map/ppermute | solution.py:22
  64.3 33.1 %collective-permute-start.4 = (f32[2,128,2,256]{1,3,2,0:T(8,128)}, f32[2,128,2,256]{1,3,2,0:T(8,128)}, u32[]{:S(2)}, u32[]{:S(2)}) collective-permute-start(f32[2,128,2,256]{1,3,2,0:T(8,128)} %get-tuple-element.44), channel_id=1, source_target_pairs={{0,1},{1,2},{2,3},{3,4},{4,5},{5,6},{6,7},{7,8},{8,9},{9,10},{10,1... | collective-permute-start | bytes 1572872 | tf_op jit(solution)/shard_map/ppermute | solution.py:12
  104.9 6.8 %collective-permute-done.5 = f32[2,128,2,256]{1,3,2,0:T(8,128)} collective-permute-done((f32[2,128,2,256]{1,3,2,0:T(8,128)}, f32[2,128,2,256]{1,3,2,0:T(8,128)}, u32[]{:S(2)}, u32[]{:S(2)}) %collective-permute-start.5) | collective-permute-done | bytes 524320 | tf_op jit(solution)/shard_map/ppermute | solution.py:12
  115.1 9.0 %collective-permute-start.6 = (f32[128,768]{0,1:T(8,128)S(1)}, f32[128,768]{0,1:T(8,128)S(1)}, u32[]{:S(2)}, u32[]{:S(2)}) collective-permute-start(f32[128,768]{0,1:T(8,128)S(1)} %convert_subtract_fusion.1), channel_id=1, source_target_pairs={{0,16},{16,0},{1,17},{17,1},{2,18},{18,2},{3,19},{19,3},{4,20},{20... | collective-permute-start | bytes 1179656 | tf_op jit(solution)/shard_map/ppermute | solution.py:22
  124.1 9.5 %collective-permute-done.6 = f32[128,768]{0,1:T(8,128)S(1)} collective-permute-done((f32[128,768]{0,1:T(8,128)S(1)}, f32[128,768]{0,1:T(8,128)S(1)}, u32[]{:S(2)}, u32[]{:S(2)}) %collective-permute-start.6) | collective-permute-done | bytes 393248 | tf_op jit(solution)/shard_map/ppermute | solution.py:22
  133.7 1.9 collective-permute-start.8
  136.0 20.9 %collective-permute-start.7 = (f32[2,128,2,256]{1,3,2,0:T(8,128)S(1)}, f32[2,128,2,256]{1,3,2,0:T(8,128)S(1)}, u32[]{:S(2)}, u32[]{:S(2)}) collective-permute-start(f32[2,128,2,256]{1,3,2,0:T(8,128)S(1)} %get-tuple-element.36), channel_id=1, source_target_pairs={{0,1},{1,2},{2,3},{3,4},{4,5},{5,6},{6,7},{7,8},{8,9},{9,10},{10,1... | collective-permute-start | bytes 1572872 | tf_op jit(solution)/shard_map/ppermute | solution.py:12
  157.7 3.8 %collective-permute-done.8 = f32[2,128,2,256]{1,3,2,0:T(8,128)S(1)} collective-permute-done((f32[2,128,2,256]{1,3,2,0:T(8,128)S(1)}, f32[2,128,2,256]{1,3,2,0:T(8,128)S(1)}, u32[]{:S(2)}, u32[]{:S(2)}) %collective-permute-start.8) | collective-permute-done | bytes 524320 | tf_op jit(solution)/shard_map/ppermute | solution.py:12
  162.0 5.0 %collective-permute-done.7 = f32[2,128,2,256]{1,3,2,0:T(8,128)S(1)} collective-permute-done((f32[2,128,2,256]{1,3,2,0:T(8,128)S(1)}, f32[2,128,2,256]{1,3,2,0:T(8,128)S(1)}, u32[]{:S(2)}, u32[]{:S(2)}) %collective-permute-start.7) | collective-permute-done | bytes 524320 | tf_op jit(solution)/shard_map/ppermute | solution.py:12
  172.4 7.4 %collective-permute-start.9 = (f32[128,768]{0,1:T(8,128)S(1)}, f32[128,768]{0,1:T(8,128)S(1)}, u32[]{:S(2)}, u32[]{:S(2)}) collective-permute-start(f32[128,768]{0,1:T(8,128)S(1)} %fusion.56), channel_id=1, source_target_pairs={{0,16},{16,0},{1,17},{17,1},{2,18},{18,2},{3,19},{19,3},{4,20},{20... | collective-permute-start | bytes 1179656 | tf_op jit(solution)/shard_map/ppermute | solution.py:22
  179.8 14.1 %collective-permute-done.9 = f32[128,768]{0,1:T(8,128)S(1)} collective-permute-done((f32[128,768]{0,1:T(8,128)S(1)}, f32[128,768]{0,1:T(8,128)S(1)}, u32[]{:S(2)}, u32[]{:S(2)}) %collective-permute-start.9) | collective-permute-done | bytes 393248 | tf_op jit(solution)/shard_map/ppermute | solution.py:22
  194.1 22.4 %collective-permute-start.10 = (f32[2,128,2,256]{1,3,2,0:T(8,128)S(1)}, f32[2,128,2,256]{1,3,2,0:T(8,128)S(1)}, u32[]{:S(2)}, u32[]{:S(2)}) collective-permute-start(f32[2,128,2,256]{1,3,2,0:T(8,128)S(1)} %get-tuple-element.28), channel_id=1, source_target_pairs={{0,1},{1,2},{2,3},{3,4},{4,5},{5,6},{6,7},{7,8},{8,9},{9,10},{10,1... | collective-permute-start | bytes 1572872 | tf_op jit(solution)/shard_map/ppermute | solution.py:12
  219.2 3.4 collective-permute-done.10
  222.7 4.3 %collective-permute-done.11 = f32[2,128,2,256]{1,3,2,0:T(8,128)S(1)} collective-permute-done((f32[2,128,2,256]{1,3,2,0:T(8,128)S(1)}, f32[2,128,2,256]{1,3,2,0:T(8,128)S(1)}, u32[]{:S(2)}, u32[]{:S(2)}) %collective-permute-start.11) | collective-permute-done | bytes 524320 | tf_op jit(solution)/shard_map/ppermute | solution.py:12
  229.1 14.1 %collective-permute-start.12 = (f32[128,768]{0,1:T(8,128)S(1)}, f32[128,768]{0,1:T(8,128)S(1)}, u32[]{:S(2)}, u32[]{:S(2)}) collective-permute-start(f32[128,768]{0,1:T(8,128)S(1)} %bitcast.770), channel_id=1, source_target_pairs={{0,16},{16,0},{1,17},{17,1},{2,18},{18,2},{3,19},{19,3},{4,20},{20... | collective-permute-start | bytes 1179656 | tf_op jit(solution)/shard_map/ppermute | solution.py:22
  243.2 5.5 %collective-permute-done.12 = f32[128,768]{0,1:T(8,128)S(1)} collective-permute-done((f32[128,768]{0,1:T(8,128)S(1)}, f32[128,768]{0,1:T(8,128)S(1)}, u32[]{:S(2)}, u32[]{:S(2)}) %collective-permute-start.12) | collective-permute-done | bytes 393248 | tf_op jit(solution)/shard_map/ppermute | solution.py:22
  248.8 26.7 %collective-permute-start.13 = (f32[2,128,2,256]{1,3,2,0:T(8,128)S(1)}, f32[2,128,2,256]{1,3,2,0:T(8,128)S(1)}, u32[]{:S(2)}, u32[]{:S(2)}) collective-permute-start(f32[2,128,2,256]{1,3,2,0:T(8,128)S(1)} %get-tuple-element.20), channel_id=1, source_target_pairs={{0,1},{1,2},{2,3},{3,4},{4,5},{5,6},{6,7},{7,8},{8,9},{9,10},{10,1... | collective-permute-start | bytes 1572872 | tf_op jit(solution)/shard_map/ppermute | solution.py:12
  275.5 1.9 collective-permute-start.14
  278.2 3.4 collective-permute-done.13
  281.7 8.5 %collective-permute-done.14 = f32[2,128,2,256]{1,3,2,0:T(8,128)S(1)} collective-permute-done((f32[2,128,2,256]{1,3,2,0:T(8,128)S(1)}, f32[2,128,2,256]{1,3,2,0:T(8,128)S(1)}, u32[]{:S(2)}, u32[]{:S(2)}) %collective-permute-start.14) | collective-permute-done | bytes 524320 | tf_op jit(solution)/shard_map/ppermute | solution.py:12
  292.5 7.6 %collective-permute-start.15 = (f32[128,768]{0,1:T(8,128)S(1)}, f32[128,768]{0,1:T(8,128)S(1)}, u32[]{:S(2)}, u32[]{:S(2)}) collective-permute-start(f32[128,768]{0,1:T(8,128)S(1)} %convert_subtract_fusion), channel_id=1, source_target_pairs={{0,16},{16,0},{1,17},{17,1},{2,18},{18,2},{3,19},{19,3},{4,20},{20... | collective-permute-start | bytes 1179656 | tf_op jit(solution)/shard_map/ppermute | solution.py:22
  300.1 16.8 %collective-permute-done.15 = f32[128,768]{0,1:T(8,128)S(1)} collective-permute-done((f32[128,768]{0,1:T(8,128)S(1)}, f32[128,768]{0,1:T(8,128)S(1)}, u32[]{:S(2)}, u32[]{:S(2)}) %collective-permute-start.15) | collective-permute-done | bytes 393248 | tf_op jit(solution)/shard_map/ppermute | solution.py:22
  317.1 18.9 %collective-permute-start.16 = (f32[2,128,2,256]{1,3,2,0:T(8,128)S(1)}, f32[2,128,2,256]{1,3,2,0:T(8,128)S(1)}, u32[]{:S(2)}, u32[]{:S(2)}) collective-permute-start(f32[2,128,2,256]{1,3,2,0:T(8,128)S(1)} %get-tuple-element.12), channel_id=1, source_target_pairs={{0,1},{1,2},{2,3},{3,4},{4,5},{5,6},{6,7},{7,8},{8,9},{9,10},{10,1... | collective-permute-start | bytes 1572872 | tf_op jit(solution)/shard_map/ppermute | solution.py:12
  336.0 2.1 collective-permute-start.17
  339.0 3.1 collective-permute-done.16
  342.2 4.3 %collective-permute-done.17 = f32[2,128,2,256]{1,3,2,0:T(8,128)S(1)} collective-permute-done((f32[2,128,2,256]{1,3,2,0:T(8,128)S(1)}, f32[2,128,2,256]{1,3,2,0:T(8,128)S(1)}, u32[]{:S(2)}, u32[]{:S(2)}) %collective-permute-start.17) | collective-permute-done | bytes 524320 | tf_op jit(solution)/shard_map/ppermute | solution.py:12
  (147 shorter events, 42.8 us)
Async XLA Ops:
  0.0 37.5 %copy-start.3 = (f32[128,768]{1,0:T(8,128)S(1)}, f32[128,768]{1,0:T(8,128)}, u32[]{:S(2)}) copy-start(f32[128,768]{1,0:T(8,128)} %param.3) | copy-start | bytes 1179652
  1.1 40.1 %copy-start = (f32[128,384]{0,1:T(8,128)}, f32[128,384]{0,1:T(8,128)S(1)}, u32[]{:S(2)}) copy-start(f32[128,384]{0,1:T(8,128)S(1)} %copy.55) | copy-start | bytes 589828
  1.1 20.0 %collective-permute-start = (f32[128,384]{0,1:T(8,128)S(1)}, f32[128,384]{0,1:T(8,128)S(1)}, u32[]{:S(2)}, u32[]{:S(2)}) collective-permute-start(f32[128,384]{0,1:T(8,128)S(1)} %copy.55), channel_id=1, source_target_pairs={{0,16},{16,0},{1,17},{17,1},{2,18},{18,2},{3,19},{19,3},{4,20},{20... | collective-permute-start | bytes 589832 | tf_op jit(solution)/shard_map/ppermute | solution.py:22
  21.2 18.4 %collective-permute-start.2 = (f32[2,128,2,128]{1,3,2,0:T(8,128)S(1)}, f32[2,128,2,128]{1,3,2,0:T(8,128)S(1)}, u32[]{:S(2)}, u32[]{:S(2)}) collective-permute-start(f32[2,128,2,128]{1,3,2,0:T(8,128)S(1)} %get-tuple-element.54), channel_id=1, source_target_pairs={{1,0},{2,1},{3,2},{4,3},{5,4},{6,5},{7,6},{8,7},{9,8},{10,9},{11,1... | collective-permute-start | bytes 786440 | tf_op jit(solution)/shard_map/ppermute | solution.py:12
  24.7 16.1 %collective-permute-start.1 = (f32[2,128,2,128]{1,3,2,0:T(8,128)S(1)}, f32[2,128,2,128]{1,3,2,0:T(8,128)S(1)}, u32[]{:S(2)}, u32[]{:S(2)}) collective-permute-start(f32[2,128,2,128]{1,3,2,0:T(8,128)S(1)} %get-tuple-element.53), channel_id=1, source_target_pairs={{0,1},{1,2},{2,3},{3,4},{4,5},{5,6},{6,7},{7,8},{8,9},{9,10},{10,1... | collective-permute-start | bytes 786440 | tf_op jit(solution)/shard_map/ppermute | solution.py:12
  41.6 15.5 %copy-start.7 = (s32[1,6]{1,0:T(1,128)S(1)}, s32[1,6]{1,0:T(1,128)}, u32[]{:S(2)}) copy-start(s32[1,6]{1,0:T(1,128)} %param.5) | copy-start | bytes 76
  43.9 14.3 %copy-start.2 = (f32[128,3,2,128]{0,3,2,1:T(8,128)}, f32[128,3,2,128]{0,3,2,1:T(8,128)S(1)}, u32[]{:S(2)}) copy-start(f32[128,3,2,128]{0,3,2,1:T(8,128)S(1)} %pad_maximum_fusion.6) | copy-start | bytes 1179652
  44.0 18.1 %collective-permute-start.3 = (f32[128,768]{0,1:T(8,128)S(1)}, f32[128,768]{0,1:T(8,128)}, u32[]{:S(2)}, u32[]{:S(2)}) collective-permute-start(f32[128,768]{0,1:T(8,128)S(1)} %bitcast.769), channel_id=1, source_target_pairs={{0,16},{16,0},{1,17},{17,1},{2,18},{18,2},{3,19},{19,3},{4,20},{20... | collective-permute-start | bytes 1179656 | tf_op jit(solution)/shard_map/ppermute | solution.py:22
  64.3 39.5 %collective-permute-start.4 = (f32[2,128,2,256]{1,3,2,0:T(8,128)}, f32[2,128,2,256]{1,3,2,0:T(8,128)}, u32[]{:S(2)}, u32[]{:S(2)}) collective-permute-start(f32[2,128,2,256]{1,3,2,0:T(8,128)} %get-tuple-element.44), channel_id=1, source_target_pairs={{0,1},{1,2},{2,3},{3,4},{4,5},{5,6},{6,7},{7,8},{8,9},{9,10},{10,1... | collective-permute-start | bytes 1572872 | tf_op jit(solution)/shard_map/ppermute | solution.py:12
  98.0 13.7 %collective-permute-start.5 = (f32[2,128,2,256]{1,3,2,0:T(8,128)}, f32[2,128,2,256]{1,3,2,0:T(8,128)}, u32[]{:S(2)}, u32[]{:S(2)}) collective-permute-start(f32[2,128,2,256]{1,3,2,0:T(8,128)} %get-tuple-element.45), channel_id=1, source_target_pairs={{1,0},{2,1},{3,2},{4,3},{5,4},{6,5},{7,6},{8,7},{9,8},{10,9},{11,1... | collective-permute-start | bytes 1572872 | tf_op jit(solution)/shard_map/ppermute | solution.py:12
  112.8 2.0 copy-start.5
  114.8 20.8 %copy-start.1 = (f32[128,384]{0,1:T(8,128)S(1)}, f32[128,384]{0,1:T(8,128)}, u32[]{:S(2)}) copy-start(f32[128,384]{0,1:T(8,128)} %copy-done) | copy-start | bytes 589828
  114.9 20.9 %copy-start.4 = (f32[3,2]{1,0:T(4,128)S(1)}, f32[3,2]{1,0:T(4,128)}, u32[]{:S(2)}) copy-start(f32[3,2]{1,0:T(4,128)} %get-tuple-element.5) | copy-start | bytes 76
  114.9 21.0 %copy-start.6 = (f32[2]{0:T(128)S(1)}, f32[2]{0:T(128)}, u32[]{:S(2)}) copy-start(f32[2]{0:T(128)} %get-tuple-element.58) | copy-start | bytes 28
  115.1 18.5 %collective-permute-start.6 = (f32[128,768]{0,1:T(8,128)S(1)}, f32[128,768]{0,1:T(8,128)S(1)}, u32[]{:S(2)}, u32[]{:S(2)}) collective-permute-start(f32[128,768]{0,1:T(8,128)S(1)} %convert_subtract_fusion.1), channel_id=1, source_target_pairs={{0,16},{16,0},{1,17},{17,1},{2,18},{18,2},{3,19},{19,3},{4,20},{20... | collective-permute-start | bytes 1179656 | tf_op jit(solution)/shard_map/ppermute | solution.py:22
  133.7 27.8 %collective-permute-start.8 = (f32[2,128,2,256]{1,3,2,0:T(8,128)S(1)}, f32[2,128,2,256]{1,3,2,0:T(8,128)S(1)}, u32[]{:S(2)}, u32[]{:S(2)}) collective-permute-start(f32[2,128,2,256]{1,3,2,0:T(8,128)S(1)} %get-tuple-element.37), channel_id=1, source_target_pairs={{1,0},{2,1},{3,2},{4,3},{5,4},{6,5},{7,6},{8,7},{9,8},{10,9},{11,1... | collective-permute-start | bytes 1572872 | tf_op jit(solution)/shard_map/ppermute | solution.py:12
  136.0 31.0 %collective-permute-start.7 = (f32[2,128,2,256]{1,3,2,0:T(8,128)S(1)}, f32[2,128,2,256]{1,3,2,0:T(8,128)S(1)}, u32[]{:S(2)}, u32[]{:S(2)}) collective-permute-start(f32[2,128,2,256]{1,3,2,0:T(8,128)S(1)} %get-tuple-element.36), channel_id=1, source_target_pairs={{0,1},{1,2},{2,3},{3,4},{4,5},{5,6},{6,7},{7,8},{8,9},{9,10},{10,1... | collective-permute-start | bytes 1572872 | tf_op jit(solution)/shard_map/ppermute | solution.py:12
  172.4 21.6 %collective-permute-start.9 = (f32[128,768]{0,1:T(8,128)S(1)}, f32[128,768]{0,1:T(8,128)S(1)}, u32[]{:S(2)}, u32[]{:S(2)}) collective-permute-start(f32[128,768]{0,1:T(8,128)S(1)} %fusion.56), channel_id=1, source_target_pairs={{0,16},{16,0},{1,17},{17,1},{2,18},{18,2},{3,19},{19,3},{4,20},{20... | collective-permute-start | bytes 1179656 | tf_op jit(solution)/shard_map/ppermute | solution.py:22
  194.1 28.5 %collective-permute-start.10 = (f32[2,128,2,256]{1,3,2,0:T(8,128)S(1)}, f32[2,128,2,256]{1,3,2,0:T(8,128)S(1)}, u32[]{:S(2)}, u32[]{:S(2)}) collective-permute-start(f32[2,128,2,256]{1,3,2,0:T(8,128)S(1)} %get-tuple-element.28), channel_id=1, source_target_pairs={{0,1},{1,2},{2,3},{3,4},{4,5},{5,6},{6,7},{7,8},{8,9},{9,10},{10,1... | collective-permute-start | bytes 1572872 | tf_op jit(solution)/shard_map/ppermute | solution.py:12
  216.5 10.5 %collective-permute-start.11 = (f32[2,128,2,256]{1,3,2,0:T(8,128)S(1)}, f32[2,128,2,256]{1,3,2,0:T(8,128)S(1)}, u32[]{:S(2)}, u32[]{:S(2)}) collective-permute-start(f32[2,128,2,256]{1,3,2,0:T(8,128)S(1)} %get-tuple-element.29), channel_id=1, source_target_pairs={{1,0},{2,1},{3,2},{4,3},{5,4},{6,5},{7,6},{8,7},{9,8},{10,9},{11,1... | collective-permute-start | bytes 1572872 | tf_op jit(solution)/shard_map/ppermute | solution.py:12
  229.1 19.6 %collective-permute-start.12 = (f32[128,768]{0,1:T(8,128)S(1)}, f32[128,768]{0,1:T(8,128)S(1)}, u32[]{:S(2)}, u32[]{:S(2)}) collective-permute-start(f32[128,768]{0,1:T(8,128)S(1)} %bitcast.770), channel_id=1, source_target_pairs={{0,16},{16,0},{1,17},{17,1},{2,18},{18,2},{3,19},{19,3},{4,20},{20... | collective-permute-start | bytes 1179656 | tf_op jit(solution)/shard_map/ppermute | solution.py:22
  248.8 32.8 %collective-permute-start.13 = (f32[2,128,2,256]{1,3,2,0:T(8,128)S(1)}, f32[2,128,2,256]{1,3,2,0:T(8,128)S(1)}, u32[]{:S(2)}, u32[]{:S(2)}) collective-permute-start(f32[2,128,2,256]{1,3,2,0:T(8,128)S(1)} %get-tuple-element.20), channel_id=1, source_target_pairs={{0,1},{1,2},{2,3},{3,4},{4,5},{5,6},{6,7},{7,8},{8,9},{9,10},{10,1... | collective-permute-start | bytes 1572872 | tf_op jit(solution)/shard_map/ppermute | solution.py:12
  275.5 14.7 %collective-permute-start.14 = (f32[2,128,2,256]{1,3,2,0:T(8,128)S(1)}, f32[2,128,2,256]{1,3,2,0:T(8,128)S(1)}, u32[]{:S(2)}, u32[]{:S(2)}) collective-permute-start(f32[2,128,2,256]{1,3,2,0:T(8,128)S(1)} %get-tuple-element.21), channel_id=1, source_target_pairs={{1,0},{2,1},{3,2},{4,3},{5,4},{6,5},{7,6},{8,7},{9,8},{10,9},{11,1... | collective-permute-start | bytes 1572872 | tf_op jit(solution)/shard_map/ppermute | solution.py:12
  292.5 24.5 %collective-permute-start.15 = (f32[128,768]{0,1:T(8,128)S(1)}, f32[128,768]{0,1:T(8,128)S(1)}, u32[]{:S(2)}, u32[]{:S(2)}) collective-permute-start(f32[128,768]{0,1:T(8,128)S(1)} %convert_subtract_fusion), channel_id=1, source_target_pairs={{0,16},{16,0},{1,17},{17,1},{2,18},{18,2},{3,19},{19,3},{4,20},{20... | collective-permute-start | bytes 1179656 | tf_op jit(solution)/shard_map/ppermute | solution.py:22
  317.1 25.0 %collective-permute-start.16 = (f32[2,128,2,256]{1,3,2,0:T(8,128)S(1)}, f32[2,128,2,256]{1,3,2,0:T(8,128)S(1)}, u32[]{:S(2)}, u32[]{:S(2)}) collective-permute-start(f32[2,128,2,256]{1,3,2,0:T(8,128)S(1)} %get-tuple-element.12), channel_id=1, source_target_pairs={{0,1},{1,2},{2,3},{3,4},{4,5},{5,6},{6,7},{7,8},{8,9},{9,10},{10,1... | collective-permute-start | bytes 1572872 | tf_op jit(solution)/shard_map/ppermute | solution.py:12
  336.0 10.5 %collective-permute-start.17 = (f32[2,128,2,256]{1,3,2,0:T(8,128)S(1)}, f32[2,128,2,256]{1,3,2,0:T(8,128)S(1)}, u32[]{:S(2)}, u32[]{:S(2)}) collective-permute-start(f32[2,128,2,256]{1,3,2,0:T(8,128)S(1)} %get-tuple-element.13), channel_id=1, source_target_pairs={{1,0},{2,1},{3,2},{4,3},{5,4},{6,5},{7,6},{8,7},{9,8},{10,9},{11,1... | collective-permute-start | bytes 1572872 | tf_op jit(solution)/shard_map/ppermute | solution.py:12
where the time goes:
time: 354 us; the launch traced here: 353 us
  starting transfers between devices  214 us (60%)
  waiting for transfers between devices  100 us (28%)
  matrix products  21.9 us (6%)
  local copies, waits for them, and re-layouts  9.46 us (3%)
  other arithmetic  6.16 us (2%)
    ppermute x12, starting transfers between devices, from_behind(): return lax.ppermute(shard, axis, pairs)  148 us
    ppermute x6, starting transfers between devices, swapped(): return lax.ppermute(block, axis, route)  66.1 us
    ppermute x6, waiting for transfers between devices, swapped(): return lax.ppermute(block, axis, route)  54.4 us
    ppermute x12, waiting for transfers between devices, from_behind(): return lax.ppermute(shard, axis, pairs)  46 us
    dot_general x42, matrix products, window_product(): lax.dot_general(left[:, slot], nearby[:, slot, :, source], (((1, 2), (0,...  16.5 us
  transfers between devices with their start and end apart: 18, of which 18 were waited for; matrix products, arithmetic and copies ran while one was open for 3% of the time, Pallas kernels for 0%

commit v1 on v0

v1 whole, which is shorter than its diff:
```python
import jax
import jax.numpy as jnp
from jax import lax
from jax.experimental import pallas as pl
from jax.experimental.pallas import tpu as pltpu
from jax.sharding import PartitionSpec as P

ITERS = 2
MESH = pl.DeviceIdType.MESH
F32 = jnp.float32
BF16 = jnp.bfloat16
B = 256
SPAN = {0: (0, 512), 1: (0, 768), 2: (256, 768)}


def split(value):
    high = value.astype(BF16)
    low = (value - high.astype(F32)).astype(BF16)
    return high, low


def dot3(left, right, nt):
    dims = (((1,), (1 if nt else 0,)), ((), ()))

    def one(x, y):
        return lax.dot_general(x, y, dims, preferred_element_type=F32)

    return one(left[0], right[0]) + one(left[0], right[1]) + one(left[1], right[0])


def make_kernel(n_blk, tile):
    own = pl.ds(B, tile)
    other = pl.ds(B + tile, tile)
    both = pl.ds(B, B)

    def col(slot, half):
        return pl.ds(slot * B + half * tile, tile)

    def cols(slot):
        return pl.ds(slot * B, B)

    def kernel(s_hbm, h_hbm, zp_ref, out_ref, sn, z0, z1, d0, d1, so_dn, so_up, sx_dn, kbuf, kx,
               s_hi, s_lo, z_hi, z_lo, d_hi, d_lo, lsem, ssem, rsem):
        side = lax.axis_index("side")
        blk = lax.axis_index("blk")
        partner = {"side": 1 - side}
        up = {"blk": blk + 1}
        dn = {"blk": blk - 1}
        has_up = blk < n_blk - 1
        has_dn = blk > 0

        barrier = pltpu.get_barrier_semaphore()
        pl.semaphore_signal(barrier, inc=1, device_id=partner, device_id_type=MESH)

        @pl.when(has_up)
        def _():
            pl.semaphore_signal(barrier, inc=1, device_id=up, device_id_type=MESH)

        @pl.when(has_dn)
        def _():
            pl.semaphore_signal(barrier, inc=1, device_id=dn, device_id_type=MESH)

        loads = []
        for e in range(3):
            loads.append(pltpu.make_async_copy(h_hbm.at[:, pl.ds(e * tile, tile)], z0.at[own, col(e, 0)], lsem.at[6 + e]))
        for e in range(3):
            for g in range(2):
                half = side if g == 0 else 1 - side
                src = s_hbm.at[:, pl.ds(pl.multiple_of((2 * e + half) * tile, tile), tile)]
                loads.append(pltpu.make_async_copy(src, sn.at[own, col(e, g)], lsem.at[2 * e + g]))
        for load in loads:
            load.start()

        keep_own = [zp_ref[0, 2 * e + (side if g == 0 else 1 - side)].astype(F32) for e in range(3) for g in range(2)]
        row_id = lax.broadcasted_iota(jnp.int32, (8, tile), 0)
        packed = jnp.zeros((8, tile), F32)
        for r in range(6):
            packed = jnp.where(row_id == r, keep_own[r], packed)
        kbuf[...] = packed

        zero = jnp.zeros((tile, tile), F32)
        for e in range(3):
            z0[own, col(e, 1)] = zero
            z0[other, col(e, 0)] = zero
        for e in (0, 1):
            z0[pl.ds(0, tile), col(e, 1)] = zero
            z0[pl.ds(tile, tile), col(e, 0)] = zero
            z0[pl.ds(2 * B, tile), col(e + 1, 1)] = zero
            z0[pl.ds(2 * B + tile, tile), col(e + 1, 0)] = zero

        @pl.when(jnp.logical_not(has_dn))
        def _():
            for e in (0, 1):
                z0[pl.ds(0, tile), col(e, 0)] = zero
                z0[pl.ds(tile, tile), col(e, 1)] = zero
                for ref in (z1, d0, d1):
                    ref[pl.ds(0, B), cols(e)] = jnp.zeros((B, B), F32)
            sn[pl.ds(0, tile), pl.ds(0, B)] = jnp.zeros((tile, B), F32)
            sn[pl.ds(tile, tile), pl.ds(tile, tile)] = zero
            so_dn[...] = zero
            sx_dn[...] = zero

        @pl.when(jnp.logical_not(has_up))
        def _():
            for e in (1, 2):
                z0[pl.ds(2 * B, tile), col(e, 0)] = zero
                z0[pl.ds(2 * B + tile, tile), col(e, 1)] = zero
                for ref in (z1, d0, d1):
                    ref[pl.ds(2 * B, B), cols(e)] = jnp.zeros((B, B), F32)
            sn[pl.ds(2 * B, tile), pl.ds(2 * B, B)] = jnp.zeros((tile, B), F32)
            sn[pl.ds(2 * B + tile, tile), pl.ds(2 * B + tile, tile)] = zero
            so_up[...] = zero

        inner = jnp.logical_and(has_up, has_dn)

        @pl.when(inner)
        def _():
            pl.semaphore_wait(barrier, 3)

        @pl.when(jnp.logical_not(inner))
        def _():
            pl.semaphore_wait(barrier, 2)

        used = []

        def remote(src, dst, where):
            i = len(used)
            copy = pltpu.make_async_remote_copy(
                src_ref=src, dst_ref=dst, send_sem=ssem.at[i], recv_sem=rsem.at[i],
                device_id={"x": partner, "u": up, "d": dn}[where], device_id_type=MESH)
            used.append((copy, where))
            return copy

        def start(ups, dns):
            if ups:
                @pl.when(has_up)
                def _():
                    for c in ups:
                        c.start()
            if dns:
                @pl.when(has_dn)
                def _():
                    for c in dns:
                        c.start()

        def receive(ups, dns):
            if ups:
                @pl.when(has_dn)
                def _():
                    for c in ups:
                        c.wait_recv()
            if dns:
                @pl.when(has_up)
                def _():
                    for c in dns:
                        c.wait_recv()

        for load in loads:
            load.wait()
        x_z = [remote(z0.at[own, col(e, 0)], z0.at[other, col(e, 1)], "x") for e in range(3)]
        x_s1 = remote(sn.at[own, col(1, 0)], sn.at[other, col(1, 1)], "x")
        x_s2 = remote(sn.at[own, col(2, 0)], sn.at[other, col(2, 1)], "x")
        x_k = remote(kbuf, kx, "x")
        for c in (x_z[1], x_z[0], x_z[2], x_s1, x_s2, x_k):
            c.start()

        lo, hi = pl.ds(0, tile), pl.ds(tile, tile)
        top, tox = pl.ds(2 * B, tile), pl.ds(2 * B + tile, tile)
        u_own = [
            remote(z0.at[own, col(1, 0)], z0.at[lo, col(0, 0)], "u"),
            remote(z0.at[own, col(2, 0)], z0.at[lo, col(1, 0)], "u"),
            remote(sn.at[own, cols(1)], sn.at[lo, cols(0)], "u"),
            remote(sn.at[own, col(2, 1)], so_dn, "u"),
        ]
        d_own = [
            remote(z0.at[own, col(0, 0)], z0.at[top, col(1, 0)], "d"),
            remote(z0.at[own, col(1, 0)], z0.at[top, col(2, 0)], "d"),
            remote(sn.at[own, cols(1)], sn.at[top, cols(2)], "d"),
            remote(sn.at[own, col(0, 1)], so_up, "d"),
        ]
        start(u_own, d_own)

        x_z[1].wait_recv()
        u_z1 = remote(z0.at[other, col(1, 1)], z0.at[hi, col(0, 1)], "u")
        d_z1 = remote(z0.at[other, col(1, 1)], z0.at[tox, col(2, 1)], "d")
        start([u_z1], [d_z1])
        x_z[0].wait_recv()
        d_z0 = remote(z0.at[other, col(0, 1)], z0.at[tox, col(1, 1)], "d")
        start([], [d_z0])
        x_z[2].wait_recv()
        u_z2 = remote(z0.at[other, col(2, 1)], z0.at[hi, col(1, 1)], "u")
        start([u_z2], [])
        x_s1.wait_recv()
        u_s1 = remote(sn.at[other, col(1, 1)], sn.at[hi, col(0, 1)], "u")
        d_s1 = remote(sn.at[other, col(1, 1)], sn.at[tox, col(2, 1)], "d")
        start([u_s1], [d_s1])
        x_s2.wait_recv()
        u_s2 = remote(sn.at[other, col(2, 1)], sx_dn, "u")
        start([u_s2], [])

        sn[other, col(1, 0)] = sn[own, col(1, 1)].T
        receive(u_own, d_own)
        sn[other, col(0, 0)] = so_dn[...].T
        sn[other, col(2, 0)] = so_up[...].T
        sn[hi, col(0, 0)] = sn[lo, col(0, 1)].T
        sn[tox, col(2, 0)] = sn[top, col(2, 1)].T
        receive([u_z1, u_z2, u_s1, u_s2], [d_z0, d_z1, d_s1])
        sn[other, col(0, 1)] = sx_dn[...].T
        x_k.wait_recv()

        def store_split(ref, rows, slots, refs):
            for slot in slots:
                high, low = split(ref[rows, cols(slot)])
                refs[0][rows, cols(slot)] = high
                refs[1][rows, cols(slot)] = low

        row0, row1, row2 = pl.ds(0, B), both, pl.ds(2 * B, B)

        def pick(refs, rows, columns):
            return refs[0][rows, columns], refs[1][rows, columns]

        def span(slot):
            low, high = SPAN[slot]
            return pl.ds(low, high - low)

        def cut(pair, slot):
            low, high = SPAN[slot]
            return pair[0][:, low:high], pair[1][:, low:high]

        s_refs, z_refs, d_refs = (s_hi, s_lo), (z_hi, z_lo), (d_hi, d_lo)
        store_split(sn, row0, (0,), s_refs)
        store_split(sn, row1, (0, 1, 2), s_refs)
        store_split(sn, row2, (2,), s_refs)

        eye = (lax.broadcasted_iota(jnp.int32, (B, B), 0) == lax.broadcasted_iota(jnp.int32, (B, B), 1)).astype(F32)

        for step in range(ITERS):
            last = step == ITERS - 1
            z, d = (z0, d0) if step == 0 else (z1, d1)
            store_split(z, row0, (0, 1), z_refs)
            store_split(z, row1, (0, 1, 2), z_refs)
            store_split(z, row2, (1, 2), z_refs)
            z_t = split(jnp.concatenate([z[pl.ds(k * B, B), cols(1)].T for k in range(3)], axis=1))
            t_parts = [
                dot3(cut(z_t, 0), pick(s_refs, span(0), cols(0)), False),
                dot3(z_t, pick(s_refs, row1, span(1)), True),
                dot3(cut(z_t, 2), pick(s_refs, span(2), cols(2)), False),
            ]
            t = split(jnp.concatenate(t_parts, axis=1))
            d[row1, cols(1)] = eye - dot3(t, pick(z_refs, span(1), cols(1)), False)
            ups = [remote(d.at[row1, cols(1)], d.at[row0, cols(0)], "u")]
            dns = [remote(d.at[row1, cols(1)], d.at[row2, cols(2)], "d")]
            start(ups, dns)
            d[row1, cols(2)] = -dot3(cut(t, 2), pick(z_refs, span(2), cols(2)), False)
            ups.append(remote(d.at[row1, cols(2)], d.at[row0, cols(1)], "u"))
            start(ups[1:], [])
            d[row1, cols(0)] = -dot3(cut(t, 0), pick(z_refs, span(0), cols(0)), False)
            dns.append(remote(d.at[row1, cols(0)], d.at[row2, cols(1)], "d"))
            start([], dns[1:])

            rows = tile if last else B
            mine = pl.ds(B, rows)
            left = pick(z_refs, mine, span(1))
            store_split(d, row1, (0, 1, 2), d_refs)
            f_mid = dot3(left, pick(d_refs, row1, span(1)), True)
            receive(ups, dns)
            store_split(d, row0, (0, 1), d_refs)
            store_split(d, row2, (1, 2), d_refs)

            def apply(pair, slot):
                return dot3(cut(pair, slot), pick(d_refs, pl.ds(slot * B, B), span(slot)), True)

            first = [apply(left, 0), f_mid, apply(left, 2)]
            pair = split(jnp.concatenate(first, axis=1))
            sends = []
            for slot in (1, 2, 0):
                second = apply(pair, slot)
                value = z[mine, cols(slot)] + 0.5 * first[slot] + 0.375 * second
                for g in range(2):
                    part = value[:tile, g * tile:(g + 1) * tile]
                    if not (slot == 1 and g == 0):
                        part = part * keep_own[2 * slot + g]
                    if last:
                        half = side if g == 0 else 1 - side
                        out_ref[:, pl.ds(pl.multiple_of((2 * slot + half) * tile, tile), tile)] = part
                    else:
                        z1[own, col(slot, g)] = part
                        part = value[tile:, g * tile:(g + 1) * tile]
                        if not (slot == 1 and g == 1):
                            r = 2 * slot + 1 - g
                            part = part * kx[r:r + 1, :]
                        z1[other, col(slot, g)] = part
                if not last:
                    ups = [] if slot == 0 else [remote(z1.at[row1, cols(slot)], z1.at[row0, cols(slot - 1)], "u")]
                    dns = [] if slot == 2 else [remote(z1.at[row1, cols(slot)], z1.at[row2, cols(slot + 1)], "d")]
                    start(ups, dns)
                    sends.append((ups, dns))
            for ups, dns in sends:
                receive(ups, dns)

        for c, where in used:
            if where == "x":
                c.wait_send()

        @pl.when(has_up)
        def _():
            for c, where in used:
                if where == "u":
                    c.wait_send()

        @pl.when(has_dn)
        def _():
            for c, where in used:
                if where == "d":
                    c.wait_send()

    return kernel


def solution(mesh):
    n_blk = mesh.shape["blk"]

    def per_device(intersect, half_factors, z_pattern):
        tile = intersect.shape[0]
        near = pltpu.VMEM((3 * B, 3 * B), F32)
        half = pltpu.VMEM((3 * B, 3 * B), BF16)
        block = pltpu.VMEM((tile, tile), F32)
        return pl.pallas_call(
            make_kernel(n_blk, tile),
            out_shape=jax.ShapeDtypeStruct(intersect.shape, F32),
            in_specs=[
                pl.BlockSpec(memory_space=pl.ANY),
                pl.BlockSpec(memory_space=pl.ANY),
                pl.BlockSpec(memory_space=pltpu.SMEM),
            ],
            out_specs=pl.BlockSpec(memory_space=pltpu.VMEM),
            scratch_shapes=[near] * 5 + [block] * 3 + [pltpu.VMEM((8, tile), F32)] * 2 + [half] * 6

            + [pltpu.SemaphoreType.DMA((9,)), pltpu.SemaphoreType.DMA((48,)), pltpu.SemaphoreType.DMA((48,))],
            compiler_params=pltpu.CompilerParams(
                collective_id=0, has_side_effects=True, vmem_limit_bytes=48 * 1024 * 1024),
            name="merge",
        )(intersect, half_factors, z_pattern)

    spec = P(("pair", "side", "blk"), None)
    return jax.shard_map(per_device, mesh=mesh, in_specs=(spec,) * 3, out_specs=spec, check_vma=False)
```

time: 354 us -> 85.4 us (0.24)
  the two profiles are of different devices: /device:TPU:15 before, /device:TPU:1 now
where the time goes in v1:
time: 85.4 us; the launch traced here: 85.1 us
  Pallas kernels  81.7 us (96%)
  local copies, waits for them, and re-layouts  3.32 us (4%)
    pallas_call x1, Pallas kernels, per_device(): pl.pallas_call(make_kernel(n_blk, tile), out_shape=jax.ShapeDtypeStruct(i...  81.7 us
    unnamed x7, local copies, waits for them, and re-layouts  3.32 us

profile of v1, /device:TPU:1, one launch (start us, length us, event | category | flops | bytes accessed | tf_op | source)
XLA Modules:
  0.0 85.1 jit_solution(13334329120592095823)
XLA Ops:
  0.0 0.0 copy-start
  0.0 1.0 %copy-done = f32[128,768]{1,0:T(8,128)S(1)} copy-done((f32[128,768]{1,0:T(8,128)S(1)}, f32[128,768]{1,0:T(8,128)}, u32[]{:S(2)}) %copy-start) | copy-done | bytes 393240
  1.0 0.0 copy-start.1
  1.0 0.9 %copy-done.1 = f32[128,384]{1,0:T(8,128)S(1)} copy-done((f32[128,384]{1,0:T(8,128)S(1)}, f32[128,384]{1,0:T(8,128)}, u32[]{:S(2)}) %copy-start.1) | copy-done | bytes 196632
  1.9 0.0 copy-start.2
  1.9 0.7 copy-done.2
  2.6 81.7 %merge.1 = f32[128,768]{1,0:T(8,128)S(1)} custom-call(f32[128,768]{1,0:T(8,128)S(1)} %copy-done, f32[128,384]{1,0:T(8,128)S(1)} %copy-done.1, s32[1,6]{1,0:T(1,128)S(1)} %copy-done.2), custom_call_target="tpu_custom_call" | custom-call | tf_op jit(solution)/shard_map/merge/pallas_call | solution.py:328
  84.3 0.7 copy.5
Async XLA Ops:
  0.0 1.0 %copy-start = (f32[128,768]{1,0:T(8,128)S(1)}, f32[128,768]{1,0:T(8,128)}, u32[]{:S(2)}) copy-start(f32[128,768]{1,0:T(8,128)} %s_hbm.1) | copy-start | bytes 1179652
  1.0 0.9 %copy-start.1 = (f32[128,384]{1,0:T(8,128)S(1)}, f32[128,384]{1,0:T(8,128)}, u32[]{:S(2)}) copy-start(f32[128,384]{1,0:T(8,128)} %h_hbm.1) | copy-start | bytes 589828
  1.9 0.7 copy-start.2

commit v2 on v1

v2 whole, which is shorter than its diff:
```python
import jax
import jax.numpy as jnp
from jax import lax
from jax.experimental import pallas as pl
from jax.experimental.pallas import tpu as pltpu
from jax.sharding import PartitionSpec as P

ITERS = 2
MESH = pl.DeviceIdType.MESH
F32 = jnp.float32
BF16 = jnp.bfloat16
B = 256


def split(value):
    high = value.astype(BF16)
    low = (value - high.astype(F32)).astype(BF16)
    return high, low


def dot3(left, right, nt):
    dims = (((1,), (1 if nt else 0,)), ((), ()))

    def one(x, y):
        return lax.dot_general(x, y, dims, preferred_element_type=F32)

    return one(left[0], right[0]) + one(left[0], right[1]) + one(left[1], right[0])


def make_kernel(n_blk, tile):
    own = pl.ds(B, tile)
    other = pl.ds(B + tile, tile)
    row0, row1, row2 = pl.ds(0, B), pl.ds(B, B), pl.ds(2 * B, B)
    rows_of = (row0, row1, row2)
    low_own, low_other = pl.ds(0, tile), pl.ds(tile, tile)
    top_own, top_other = pl.ds(2 * B, tile), pl.ds(2 * B + tile, tile)

    def col(slot, half):
        return pl.ds(slot * B + half * tile, tile)

    def cols(slot):
        return pl.ds(slot * B, B)

    def kernel(s_hbm, h_hbm, zp_hbm, out_ref, sn, z0, z1, d0, d1, so_dn, so_up, sx_dn, kbuf, kx,
               s_hi, s_lo, z_hi, z_lo, d_hi, d_lo, zp_ref, lsem, ssem, rsem):
        side = lax.axis_index("side")
        blk = lax.axis_index("blk")
        partner = {"side": 1 - side}
        up = {"blk": blk + 1}
        dn = {"blk": blk - 1}
        has_up = blk < n_blk - 1
        has_dn = blk > 0

        barrier = pltpu.get_barrier_semaphore()
        pl.semaphore_signal(barrier, inc=1, device_id=partner, device_id_type=MESH)

        @pl.when(has_up)
        def _():
            pl.semaphore_signal(barrier, inc=1, device_id=up, device_id_type=MESH)

        @pl.when(has_dn)
        def _():
            pl.semaphore_signal(barrier, inc=1, device_id=dn, device_id_type=MESH)

        def half_of(g):
            return side if g == 0 else 1 - side

        h_loads = [
            pltpu.make_async_copy(h_hbm.at[:, pl.ds(e * tile, tile)], z0.at[own, col(e, 0)], lsem.at[6 + e])
            for e in range(3)
        ]
        s_loads = []
        for e in range(3):
            for g in range(2):
                src = s_hbm.at[:, pl.ds(pl.multiple_of((2 * e + half_of(g)) * tile, tile), tile)]
                s_loads.append(pltpu.make_async_copy(src, sn.at[own, col(e, g)], lsem.at[2 * e + g]))
        zp_load = pltpu.make_async_copy(zp_hbm, zp_ref, lsem.at[9])
        for load in h_loads + s_loads + [zp_load]:
            load.start()
        for load in h_loads + s_loads:
            load.wait()

        inner = jnp.logical_and(has_up, has_dn)

        @pl.when(inner)
        def _():
            pl.semaphore_wait(barrier, 3)

        @pl.when(jnp.logical_not(inner))
        def _():
            pl.semaphore_wait(barrier, 2)

        used = []

        def remote(src, dst, where):
            i = len(used)
            copy = pltpu.make_async_remote_copy(
                src_ref=src, dst_ref=dst, send_sem=ssem.at[i], recv_sem=rsem.at[i],
                device_id={"x": partner, "u": up, "d": dn}[where], device_id_type=MESH)
            used.append((copy, where))
            return copy

        def start(ups, dns):
            if ups:
                @pl.when(has_up)
                def _():
                    for c in ups:
                        c.start()
            if dns:
                @pl.when(has_dn)
                def _():
                    for c in dns:
                        c.start()

        def receive(ups, dns):
            if ups:
                @pl.when(has_dn)
                def _():
                    for c in ups:
                        c.wait_recv()
            if dns:
                @pl.when(has_up)
                def _():
                    for c in dns:
                        c.wait_recv()

        x_z = [remote(z0.at[own, col(e, 0)], z0.at[other, col(e, 1)], "x") for e in range(3)]
        x_s1 = remote(sn.at[own, col(1, 0)], sn.at[other, col(1, 1)], "x")
        x_s2 = remote(sn.at[own, col(2, 0)], sn.at[other, col(2, 1)], "x")
        x_k = remote(kbuf, kx, "x")
        for c in (x_z[0], x_z[2], x_s1, x_s2, x_z[1]):
            c.start()

        u_own = [
            remote(z0.at[own, col(2, 0)], z0.at[low_own, col(1, 0)], "u"),
            remote(sn.at[own, cols(1)], sn.at[low_own, cols(0)], "u"),
            remote(sn.at[own, col(2, 1)], so_dn, "u"),
            remote(z0.at[own, col(1, 0)], z0.at[low_own, col(0, 0)], "u"),
        ]
        d_own = [
            remote(z0.at[own, col(0, 0)], z0.at[top_own, col(1, 0)], "d"),
            remote(sn.at[own, cols(1)], sn.at[top_own, cols(2)], "d"),
            remote(sn.at[own, col(0, 1)], so_up, "d"),
            remote(z0.at[own, col(1, 0)], z0.at[top_own, col(2, 0)], "d"),
        ]
        start(u_own, d_own)

        zp_load.wait()
        keep_own = [zp_ref[0, 2 * e + half_of(g)].astype(F32) for e in range(3) for g in range(2)]
        row_id = lax.broadcasted_iota(jnp.int32, (8, tile), 0)
        packed = jnp.zeros((8, tile), F32)
        for r in range(6):
            packed = jnp.where(row_id == r, keep_own[r], packed)
        kbuf[...] = packed

        zero = jnp.zeros((tile, tile), F32)
        for e in range(3):
            z0[own, col(e, 1)] = zero
            z0[other, col(e, 0)] = zero
        for e in (0, 1):
            z0[low_own, col(e, 1)] = zero
            z0[low_other, col(e, 0)] = zero
            z0[top_own, col(e + 1, 1)] = zero
            z0[top_other, col(e + 1, 0)] = zero

        @pl.when(jnp.logical_not(has_dn))
        def _():
            for e in (0, 1):
                z0[low_own, col(e, 0)] = zero
                z0[low_other, col(e, 1)] = zero
                for ref in (z1, d0, d1):
                    ref[row0, cols(e)] = jnp.zeros((B, B), F32)
            sn[low_own, cols(0)] = jnp.zeros((tile, B), F32)
            sn[low_other, col(0, 1)] = zero
            so_dn[...] = zero
            sx_dn[...] = zero

        @pl.when(jnp.logical_not(has_up))
        def _():
            for e in (1, 2):
                z0[top_own, col(e, 0)] = zero
                z0[top_other, col(e, 1)] = zero
                for ref in (z1, d0, d1):
                    ref[row2, cols(e)] = jnp.zeros((B, B), F32)
            sn[top_own, cols(2)] = jnp.zeros((tile, B), F32)
            sn[top_other, col(2, 1)] = zero
            so_up[...] = zero

        x_k.start()

        s_refs, z_refs, d_refs = (s_hi, s_lo), (z_hi, z_lo), (d_hi, d_lo)

        def keep_split(refs, row, slot, value):
            high, low = split(value)
            refs[0][rows_of[row], cols(slot)] = high
            refs[1][rows_of[row], cols(slot)] = low

        def load_split(ref, refs, places):
            for row, slot in places:
                keep_split(refs, row, slot, ref[rows_of[row], cols(slot)])

        def pick(refs, rows, columns):
            return refs[0][rows, columns], refs[1][rows, columns]

        def near(refs, row, slot):
            return pick(refs, rows_of[row], cols(slot))

        def nn(left, right):
            return dot3(left, right, False)

        def nt(left, right):
            return dot3(left, right, True)

        sn[other, col(1, 0)] = sn[own, col(1, 1)].T
        x_z[0].wait_recv()
        d_z0 = remote(z0.at[other, col(0, 1)], z0.at[top_other, col(1, 1)], "d")
        start([], [d_z0])
        x_z[2].wait_recv()
        u_z2 = remote(z0.at[other, col(2, 1)], z0.at[low_other, col(1, 1)], "u")
        start([u_z2], [])
        x_s1.wait_recv()
        u_s1 = remote(sn.at[other, col(1, 1)], sn.at[low_other, col(0, 1)], "u")
        d_s1 = remote(sn.at[other, col(1, 1)], sn.at[top_other, col(2, 1)], "d")
        start([u_s1], [d_s1])
        x_s2.wait_recv()
        u_s2 = remote(sn.at[other, col(2, 1)], sx_dn, "u")
        start([u_s2], [])
        x_z[1].wait_recv()
        u_z1 = remote(z0.at[other, col(1, 1)], z0.at[low_other, col(0, 1)], "u")
        d_z1 = remote(z0.at[other, col(1, 1)], z0.at[top_other, col(2, 1)], "d")
        start([u_z1], [d_z1])
        load_split(z0, z_refs, ((1, 0), (1, 1), (1, 2)))
        load_split(sn, s_refs, ((1, 1),))

        receive(u_own, d_own)
        sn[other, col(0, 0)] = so_dn[...].T
        sn[other, col(2, 0)] = so_up[...].T
        sn[low_other, col(0, 0)] = sn[low_own, col(0, 1)].T
        sn[top_other, col(2, 0)] = sn[top_own, col(2, 1)].T
        load_split(sn, s_refs, ((1, 2),))
        receive([u_z2, u_s1], [d_z0, d_s1])
        load_split(sn, s_refs, ((0, 0), (2, 2)))
        receive([u_s2], [])
        sn[other, col(0, 1)] = sx_dn[...].T
        load_split(sn, s_refs, ((1, 0),))
        ups, dns = [u_z1], [d_z1]

        eye = (lax.broadcasted_iota(jnp.int32, (B, B), 0) == lax.broadcasted_iota(jnp.int32, (B, B), 1)).astype(F32)

        for step in range(ITERS):
            last = step == ITERS - 1
            z, d = (z0, d0) if step == 0 else (z1, d1)

            mid = split(z[row1, cols(1)].T)
            t_own = [nn(mid, near(s_refs, 1, 0)), nt(mid, near(s_refs, 1, 1)), nn(mid, near(s_refs, 1, 2))]
            if step > 0:
                receive(*edge)
            load_split(z, z_refs, ((0, 1), (2, 1)))
            lower = split(z[row0, cols(1)].T)
            upper = split(z[row2, cols(1)].T)
            t = [
                split(t_own[0] + nn(lower, near(s_refs, 0, 0))),
                split(t_own[1] + nt(lower, near(s_refs, 1, 0)) + nt(upper, near(s_refs, 1, 2))),
                split(t_own[2] + nn(upper, near(s_refs, 2, 2))),
            ]
            value = eye - (nn(t[0], near(z_refs, 0, 1)) + nn(t[1], near(z_refs, 1, 1)) + nn(t[2], near(z_refs, 2, 1)))
            d[row1, cols(1)] = value
            u_diag = [
                remote(d.at[own, cols(1)], d.at[low_own, cols(0)], "u"),
                remote(d.at[other, col(1, 1)], d.at[low_other, col(0, 1)], "u"),
            ]
            d_diag = [
                remote(d.at[own, cols(1)], d.at[top_own, cols(2)], "d"),
                remote(d.at[other, col(1, 1)], d.at[top_other, col(2, 1)], "d"),
            ]
            start(u_diag, d_diag)
            keep_split(d_refs, 1, 1, value)

            receive(ups, dns)
            load_split(z, z_refs, ((0, 0), (2, 2)))
            value = -(nn(t[1], near(z_refs, 1, 2)) + nn(t[2], near(z_refs, 2, 2)))
            d[row1, cols(2)] = value
            u_edge = remote(d.at[row1, cols(2)], d.at[row0, cols(1)], "u")
            start([u_edge], [])
            keep_split(d_refs, 1, 2, value)
            value = -(nn(t[0], near(z_refs, 0, 0)) + nn(t[1], near(z_refs, 1, 0)))
            d[row1, cols(0)] = value
            d_edge = remote(d.at[row1, cols(0)], d.at[row2, cols(1)], "d")
            start([], [d_edge])
            keep_split(d_refs, 1, 0, value)

            mine = own if last else row1
            left = [pick(z_refs, mine, cols(k)) for k in range(3)]
            first = [None, None, None]
            first[1] = sum(nt(left[k], near(d_refs, 1, k)) for k in range(3))
            f_mid = split(first[1])
            second_mid = nt(f_mid, near(d_refs, 1, 1))
            receive(u_diag, d_diag)
            d[low_other, col(0, 0)] = d[low_own, col(0, 1)].T
            d[top_other, col(2, 0)] = d[top_own, col(2, 1)].T
            load_split(d, d_refs, ((0, 0), (2, 2)))
            first[0] = nt(left[0], near(d_refs, 0, 0))
            first[2] = nt(left[2], near(d_refs, 2, 2))
            if step == 0:
                x_k.wait_recv()

            def finish(slot, second):
                value = z[mine, cols(slot)] + 0.5 * first[slot] + 0.375 * second
                for g in range(2):
                    part = value[:tile, g * tile:(g + 1) * tile]
                    if not (slot == 1 and g == 0):
                        part = part * keep_own[2 * slot + g]
                    if last:
                        out_ref[:, pl.ds(pl.multiple_of((2 * slot + half_of(g)) * tile, tile), tile)] = part
                        continue
                    z1[own, col(slot, g)] = part
                    part = value[tile:, g * tile:(g + 1) * tile]
                    if not (slot == 1 and g == 1):
                        r = 2 * slot + 1 - g
                        part = part * kx[r:r + 1, :]
                    z1[other, col(slot, g)] = part

            receive([u_edge], [])
            load_split(d, d_refs, ((0, 1),))
            first[0] = first[0] + nt(left[1], near(d_refs, 0, 1))
            f_low = split(first[0])
            finish(0, nt(f_low, near(d_refs, 0, 0)) + nt(f_mid, near(d_refs, 0, 1)))
            edge = [[], []]
            if not last:
                edge[1].append(remote(z1.at[row1, cols(0)], z1.at[row2, cols(1)], "d"))
                start([], edge[1])
            receive([], [d_edge])
            load_split(d, d_refs, ((2, 1),))
            first[2] = first[2] + nt(left[1], near(d_refs, 2, 1))
            f_high = split(first[2])
            finish(2, nt(f_mid, near(d_refs, 2, 1)) + nt(f_high, near(d_refs, 2, 2)))
            if not last:
                edge[0].append(remote(z1.at[row1, cols(2)], z1.at[row0, cols(1)], "u"))
                start(edge[0], [])
            finish(1, second_mid + nt(f_low, near(d_refs, 1, 0)) + nt(f_high, near(d_refs, 1, 2)))
            if not last:
                ups = [remote(z1.at[row1, cols(1)], z1.at[row0, cols(0)], "u")]
                dns = [remote(z1.at[row1, cols(1)], z1.at[row2, cols(2)], "d")]
                start(ups, dns)
                load_split(z1, z_refs, ((1, 0), (1, 1), (1, 2)))

        for c, where in used:
            if where == "x":
                c.wait_send()

        @pl.when(has_up)
        def _():
            for c, where in used:
                if where == "u":
                    c.wait_send()

        @pl.when(has_dn)
        def _():
            for c, where in used:
                if where == "d":
                    c.wait_send()

    return kernel


def solution(mesh):
    n_blk = mesh.shape["blk"]

    def per_device(intersect, half_factors, z_pattern):
        tile = intersect.shape[0]
        near = pltpu.VMEM((3 * B, 3 * B), F32)
        half = pltpu.VMEM((3 * B, 3 * B), BF16)
        block = pltpu.VMEM((tile, tile), F32)
        return pl.pallas_call(
            make_kernel(n_blk, tile),
            out_shape=jax.ShapeDtypeStruct(intersect.shape, F32),
            in_specs=[
                pl.BlockSpec(memory_space=pltpu.HBM),
                pl.BlockSpec(memory_space=pltpu.HBM),
                pl.BlockSpec(memory_space=pltpu.HBM),
            ],
            out_specs=pl.BlockSpec(memory_space=pltpu.VMEM),
            scratch_shapes=[near] * 5 + [block] * 3 + [pltpu.VMEM((8, tile), F32)] * 2 + [half] * 6

            + [pltpu.SMEM((1, 6), jnp.int32), pltpu.SemaphoreType.DMA((10,)), pltpu.SemaphoreType.DMA((48,)), pltpu.SemaphoreType.DMA((48,))],
            compiler_params=pltpu.CompilerParams(
                collective_id=0, has_side_effects=True, vmem_limit_bytes=48 * 1024 * 1024),
            name="merge",
        )(intersect, half_factors, z_pattern)

    spec = P(("pair", "side", "blk"), None)
    return jax.shard_map(per_device, mesh=mesh, in_specs=(spec,) * 3, out_specs=spec, check_vma=False)
```

time: 85.4 us -> 78.4 us (0.918)
  Pallas kernels: 81.7 us -> 74.8 us
    pallas_call x1, Pallas kernels: 81.7 us -> 74.8 us  [per_device(): pl.pallas_call(make_kernel(n_blk, tile), out_shape=jax.ShapeDtypeStruct(i...]
where the time goes in v2:
time: 78.4 us; the launch traced here: 78.2 us
  Pallas kernels  74.8 us (95%)
  local copies, waits for them, and re-layouts  3.32 us (4%)
    pallas_call x1, Pallas kernels, per_device(): pl.pallas_call(make_kernel(n_blk, tile), out_shape=jax.ShapeDtypeStruct(i...  74.8 us
    unnamed x7, local copies, waits for them, and re-layouts  3.32 us

profile of v2, /device:TPU:1, one launch (start us, length us, event | category | flops | bytes accessed | tf_op | source)
XLA Modules:
  0.0 78.2 jit_solution(1296244614988873180)
XLA Ops:
  0.0 0.0 copy-start
  0.0 1.0 %copy-done = f32[128,768]{1,0:T(8,128)S(1)} copy-done((f32[128,768]{1,0:T(8,128)S(1)}, f32[128,768]{1,0:T(8,128)}, u32[]{:S(2)}) %copy-start) | copy-done | bytes 393240
  1.0 0.0 copy-start.1
  1.0 0.9 %copy-done.1 = f32[128,384]{1,0:T(8,128)S(1)} copy-done((f32[128,384]{1,0:T(8,128)S(1)}, f32[128,384]{1,0:T(8,128)}, u32[]{:S(2)}) %copy-start.1) | copy-done | bytes 196632
  1.9 0.0 copy-start.2
  1.9 0.7 copy-done.2
  2.6 74.8 %merge.1 = f32[128,768]{1,0:T(8,128)S(1)} custom-call(f32[128,768]{1,0:T(8,128)S(1)} %copy-done, f32[128,384]{1,0:T(8,128)S(1)} %copy-done.1, s32[1,6]{1,0:T(1,128)S(1)} %copy-done.2), custom_call_target="tpu_custom_call" | custom-call | tf_op jit(solution)/shard_map/merge/pallas_call | solution.py:374
  77.4 0.7 copy.5
Async XLA Ops:
  0.0 1.0 %copy-start = (f32[128,768]{1,0:T(8,128)S(1)}, f32[128,768]{1,0:T(8,128)}, u32[]{:S(2)}) copy-start(f32[128,768]{1,0:T(8,128)} %s_hbm.1) | copy-start | bytes 1179652
  1.0 0.9 %copy-start.1 = (f32[128,384]{1,0:T(8,128)S(1)}, f32[128,384]{1,0:T(8,128)}, u32[]{:S(2)}) copy-start(f32[128,384]{1,0:T(8,128)} %h_hbm.1) | copy-start | bytes 589828
  1.9 0.7 copy-start.2

commit v3 on v2

--- a/solution.py
+++ b/solution.py
@@ -16,6 +16,26 @@
     high = value.astype(BF16)
     low = (value - high.astype(F32)).astype(BF16)
     return high, low
+
+
+def lanes(shape):
+    return lax.broadcasted_iota(jnp.int32, shape, 1)
+
+
+def store_packed(ref, start, tile):
+    ref[pl.ds(start, 32), :] = tile[0:32]
+    ref[pl.ds(start + 32, 32), :] = jnp.where(lanes((32, 128)) < 32, pltpu.roll(tile[96:128], 32, 1), tile[32:64])
+    ref[pl.ds(start + 64, 16), :] = jnp.where(lanes((16, 128)) < 64, pltpu.roll(tile[80:96], 64, 1), tile[64:80])
+
+
+def load_packed(ref, start):
+    first = ref[pl.ds(start, 32), :]
+    second = ref[pl.ds(start + 32, 32), :]
+    third = ref[pl.ds(start + 64, 16), :]
+    upper = jnp.concatenate(
+        [first, second, third, pltpu.roll(third, 64, 1), pltpu.roll(second, 96, 1)], axis=0)
+    row = lax.broadcasted_iota(jnp.int32, (128, 128), 0)
+    return jnp.where(lanes((128, 128)) >= row, upper, upper.T)
 
 
 def dot3(left, right, nt):
@@ -41,7 +61,8 @@
     def cols(slot):
         return pl.ds(slot * B, B)
 
-    def kernel(s_hbm, h_hbm, zp_hbm, out_ref, sn, z0, z1, d0, d1, so_dn, so_up, sx_dn, kbuf, kx,
+    def kernel(s_hbm, h_hbm, zp_hbm, out_ref, sn, z0, z1, d0, d1, so_dn, so_up, sx_dn, sp, sx, spo_dn, spo_up, spx_dn, spx_up,
+               pd0, pd1, qdn0, qdn1, qup0, qup1, kbuf, kx,
                s_hi, s_lo, z_hi, z_lo, d_hi, d_lo, zp_ref, lsem, ssem, rsem):
         side = lax.axis_index("side")
         blk = lax.axis_index("blk")
@@ -125,21 +146,26 @@
                         c.wait_recv()
 
         x_z = [remote(z0.at[own, col(e, 0)], z0.at[other, col(e, 1)], "x") for e in range(3)]
-        x_s1 = remote(sn.at[own, col(1, 0)], sn.at[other, col(1, 1)], "x")
+        x_s1 = remote(sp, sx, "x")
         x_s2 = remote(sn.at[own, col(2, 0)], sn.at[other, col(2, 1)], "x")
         x_k = remote(kbuf, kx, "x")
-        for c in (x_z[0], x_z[2], x_s1, x_s2, x_z[1]):
+        for c in (x_z[0], x_z[2], x_s2):
             c.start()
+        store_packed(sp, 0, sn[own, col(1, 0)])
+        x_s1.start()
+        x_z[1].start()
 
         u_own = [
             remote(z0.at[own, col(2, 0)], z0.at[low_own, col(1, 0)], "u"),
-            remote(sn.at[own, cols(1)], sn.at[low_own, cols(0)], "u"),
+            remote(sp, spo_dn, "u"),
+            remote(sn.at[own, col(1, 1)], sn.at[low_own, col(0, 1)], "u"),
             remote(sn.at[own, col(2, 1)], so_dn, "u"),
             remote(z0.at[own, col(1, 0)], z0.at[low_own, col(0, 0)], "u"),
         ]
         d_own = [
             remote(z0.at[own, col(0, 0)], z0.at[top_own, col(1, 0)], "d"),
-            remote(sn.at[own, cols(1)], sn.at[top_own, cols(2)], "d"),
+            remote(sp, spo_up, "d"),
+            remote(sn.at[own, col(1, 1)], sn.at[top_own, col(2, 1)], "d"),
             remote(sn.at[own, col(0, 1)], so_up, "d"),
             remote(z0.at[own, col(1, 0)], z0.at[top_own, col(2, 0)], "d"),
         ]
@@ -168,10 +194,12 @@
             for e in (0, 1):
                 z0[low_own, col(e, 0)] = zero
                 z0[low_other, col(e, 1)] = zero
-                for ref in (z1, d0, d1):
-                    ref[row0, cols(e)] = jnp.zeros((B, B), F32)
-            sn[low_own, cols(0)] = jnp.zeros((tile, B), F32)
-            sn[low_other, col(0, 1)] = zero
+                z1[row0, cols(e)] = jnp.zeros((B, B), F32)
+            for ref in (d0, d1):
+                ref[row0, cols(1)] = jnp.zeros((B, B), F32)
+            for ref in (spo_dn, spx_dn, qdn0, qdn1):
+                ref[...] = jnp.zeros(ref.shape, F32)
+            sn[low_own, col(0, 1)] = zero
             so_dn[...] = zero
             sx_dn[...] = zero
 
@@ -180,10 +208,12 @@
             for e in (1, 2):
                 z0[top_own, col(e, 0)] = zero
                 z0[top_other, col(e, 1)] = zero
-                for ref in (z1, d0, d1):
-                    ref[row2, cols(e)] = jnp.zeros((B, B), F32)
-            sn[top_own, cols(2)] = jnp.zeros((tile, B), F32)
-            sn[top_other, col(2, 1)] = zero
+                z1[row2, cols(e)] = jnp.zeros((B, B), F32)
+            for ref in (d0, d1):
+                ref[row2, cols(1)] = jnp.zeros((B, B), F32)
+            for ref in (spo_up, spx_up, qup0, qup1):
+                ref[...] = jnp.zeros(ref.shape, F32)
+            sn[top_own, col(2, 1)] = zero
             so_up[...] = zero
 
         x_k.start()
@@ -218,31 +248,40 @@
         x_z[2].wait_recv()
         u_z2 = remote(z0.at[other, col(2, 1)], z0.at[low_other, col(1, 1)], "u")
         start([u_z2], [])
-        x_s1.wait_recv()
-        u_s1 = remote(sn.at[other, col(1, 1)], sn.at[low_other, col(0, 1)], "u")
-        d_s1 = remote(sn.at[other, col(1, 1)], sn.at[top_other, col(2, 1)], "d")
-        start([u_s1], [d_s1])
         x_s2.wait_recv()
         u_s2 = remote(sn.at[other, col(2, 1)], sx_dn, "u")
         start([u_s2], [])
+        x_s1.wait_recv()
+        u_s1 = remote(sx, spx_dn, "u")
+        d_s1 = remote(sx, spx_up, "d")
+        start([u_s1], [d_s1])
+        sn[other, col(1, 1)] = load_packed(sx, 0)
+        load_split(sn, s_refs, ((1, 1),))
+
+        receive(u_own, d_own)
+        sn[other, col(0, 0)] = so_dn[...].T
+        sn[other, col(2, 0)] = so_up[...].T
+        sn[low_own, col(0, 0)] = load_packed(spo_dn, 0)
+        sn[top_own, col(2, 0)] = load_packed(spo_up, 0)
+        sn[low_other, col(0, 0)] = sn[low_own, col(0, 1)].T
+        sn[top_other, col(2, 0)] = sn[top_own, col(2, 1)].T
+        load_split(sn, s_refs, ((1, 2),))
+        receive([u_z2], [d_z0])
+        load_split(z0, z_refs, ((0, 1), (2, 1), (1, 0), (1, 2)))
+        lower = split(z0[row0, cols(1)].T)
+        upper = split(z0[row2, cols(1)].T)
+
         x_z[1].wait_recv()
         u_z1 = remote(z0.at[other, col(1, 1)], z0.at[low_other, col(0, 1)], "u")
         d_z1 = remote(z0.at[other, col(1, 1)], z0.at[top_other, col(2, 1)], "d")
         start([u_z1], [d_z1])
-        load_split(z0, z_refs, ((1, 0), (1, 1), (1, 2)))
-        load_split(sn, s_refs, ((1, 1),))
-
-        receive(u_own, d_own)
-        sn[other, col(0, 0)] = so_dn[...].T
-        sn[other, col(2, 0)] = so_up[...].T
-        sn[low_other, col(0, 0)] = sn[low_own, col(0, 1)].T
-        sn[top_other, col(2, 0)] = sn[top_own, col(2, 1)].T
-        load_split(sn, s_refs, ((1, 2),))
-        receive([u_z2, u_s1], [d_z0, d_s1])
-        load_split(sn, s_refs, ((0, 0), (2, 2)))
-        receive([u_s2], [])
+        load_split(z0, z_refs, ((1, 1),))
+        receive([u_s2, u_s1], [d_s1])
         sn[other, col(0, 1)] = sx_dn[...].T
         load_split(sn, s_refs, ((1, 0),))
+        sn[low_other, col(0, 1)] = load_packed(spx_dn, 0)
+        sn[top_other, col(2, 1)] = load_packed(spx_up, 0)
+        load_split(sn, s_refs, ((0, 0), (2, 2)))
         ups, dns = [u_z1], [d_z1]
 
         eye = (lax.broadcasted_iota(jnp.int32, (B, B), 0) == lax.broadcasted_iota(jnp.int32, (B, B), 1)).astype(F32)
@@ -250,29 +289,25 @@
         for step in range(ITERS):
             last = step == ITERS - 1
             z, d = (z0, d0) if step == 0 else (z1, d1)
+            pd, q_dn, q_up = (pd0, qdn0, qup0) if step == 0 else (pd1, qdn1, qup1)
 
             mid = split(z[row1, cols(1)].T)
             t_own = [nn(mid, near(s_refs, 1, 0)), nt(mid, near(s_refs, 1, 1)), nn(mid, near(s_refs, 1, 2))]
             if step > 0:
                 receive(*edge)
-            load_split(z, z_refs, ((0, 1), (2, 1)))
-            lower = split(z[row0, cols(1)].T)
-            upper = split(z[row2, cols(1)].T)
+                load_split(z, z_refs, ((0, 1), (2, 1)))
+                lower = split(z[row0, cols(1)].T)
+                upper = split(z[row2, cols(1)].T)
             t = [
                 split(t_own[0] + nn(lower, near(s_refs, 0, 0))),
                 split(t_own[1] + nt(lower, near(s_refs, 1, 0)) + nt(upper, near(s_refs, 1, 2))),
                 split(t_own[2] + nn(upper, near(s_refs, 2, 2))),
             ]
             value = eye - (nn(t[0], near(z_refs, 0, 1)) + nn(t[1], near(z_refs, 1, 1)) + nn(t[2], near(z_refs, 2, 1)))
-            d[row1, cols(1)] = value
-            u_diag = [
-                remote(d.at[own, cols(1)], d.at[low_own, cols(0)], "u"),
-                remote(d.at[other, col(1, 1)], d.at[low_other, col(0, 1)], "u"),
-            ]
-            d_diag = [
-                remote(d.at[own, cols(1)], d.at[top_own, cols(2)], "d"),
-                remote(d.at[other, col(1, 1)], d.at[top_other, col(2, 1)], "d"),
-            ]
+            store_packed(pd, 0, value[:tile, :tile])
+            pd[pl.ds(80, tile), :] = value[:tile, tile:]
+            store_packed(pd, 80 + tile, value[tile:, tile:])
+            u_diag, d_diag = [remote(pd, q_dn, "u")], [remote(pd, q_up, "d")]
             start(u_diag, d_diag)
             keep_split(d_refs, 1, 1, value)
 
@@ -296,9 +331,11 @@
             f_mid = split(first[1])
             second_mid = nt(f_mid, near(d_refs, 1, 1))
             receive(u_diag, d_diag)
-            d[low_other, col(0, 0)] = d[low_own, col(0, 1)].T
-            d[top_other, col(2, 0)] = d[top_own, col(2, 1)].T
-            load_split(d, d_refs, ((0, 0), (2, 2)))
+            for row, ref in ((0, q_dn), (2, q_up)):
+                cross = ref[pl.ds(80, tile), :]
+                top = jnp.concatenate([load_packed(ref, 0), cross], axis=1)
+                low = jnp.concatenate([cross.T, load_packed(ref, 80 + tile)], axis=1)
+                keep_split(d_refs, row, row, jnp.concatenate([top, low], axis=0))
             first[0] = nt(left[0], near(d_refs, 0, 0))
             first[2] = nt(left[2], near(d_refs, 2, 2))
             if step == 0:
@@ -371,6 +408,8 @@
         near = pltpu.VMEM((3 * B, 3 * B), F32)
         half = pltpu.VMEM((3 * B, 3 * B), BF16)
         block = pltpu.VMEM((tile, tile), F32)
+        packed = pltpu.VMEM((80, tile), F32)
+        message = pltpu.VMEM((160 + tile, tile), F32)
         return pl.pallas_call(
             make_kernel(n_blk, tile),
             out_shape=jax.ShapeDtypeStruct(intersect.shape, F32),
@@ -380,7 +419,7 @@
                 pl.BlockSpec(memory_space=pltpu.HBM),
             ],
             out_specs=pl.BlockSpec(memory_space=pltpu.VMEM),
-            scratch_shapes=[near] * 5 + [block] * 3 + [pltpu.VMEM((8, tile), F32)] * 2 + [half] * 6
+            scratch_shapes=[near] * 5 + [block] * 3 + [packed] * 6 + [message] * 6 + [pltpu.VMEM((8, tile), F32)] * 2 + [half] * 6
 
             + [pltpu.SMEM((1, 6), jnp.int32), pltpu.SemaphoreType.DMA((10,)), pltpu.SemaphoreType.DMA((48,)), pltpu.SemaphoreType.DMA((48,))],
             compiler_params=pltpu.CompilerParams(

time: 78.4 us -> 76.3 us (0.973)
  Pallas kernels: 74.8 us -> 72.8 us
    pallas_call x1, Pallas kernels: 74.8 us -> 72.8 us  [per_device(): pl.pallas_call(make_kernel(n_blk, tile), out_shape=jax.ShapeDtypeStruct(i...]
where the time goes in v3:
time: 76.3 us; the launch traced here: 76.1 us
  Pallas kernels  72.8 us (95%)
  local copies, waits for them, and re-layouts  3.32 us (4%)
    pallas_call x1, Pallas kernels, per_device(): pl.pallas_call(make_kernel(n_blk, tile), out_shape=jax.ShapeDtypeStruct(i...  72.8 us
    unnamed x7, local copies, waits for them, and re-layouts  3.32 us

profile of v3, /device:TPU:1, one launch (start us, length us, event | category | flops | bytes accessed | tf_op | source)
XLA Modules:
  0.0 76.1 jit_solution(11465410970441147270)
XLA Ops:
  0.0 0.0 copy-start
  0.0 1.0 %copy-done = f32[128,768]{1,0:T(8,128)S(1)} copy-done((f32[128,768]{1,0:T(8,128)S(1)}, f32[128,768]{1,0:T(8,128)}, u32[]{:S(2)}) %copy-start) | copy-done | bytes 393240
  1.0 0.0 copy-start.1
  1.0 0.9 %copy-done.1 = f32[128,384]{1,0:T(8,128)S(1)} copy-done((f32[128,384]{1,0:T(8,128)S(1)}, f32[128,384]{1,0:T(8,128)}, u32[]{:S(2)}) %copy-start.1) | copy-done | bytes 196632
  1.9 0.0 copy-start.2
  1.9 0.7 copy-done.2
  2.6 72.8 %merge.1 = f32[128,768]{1,0:T(8,128)S(1)} custom-call(f32[128,768]{1,0:T(8,128)S(1)} %copy-done, f32[128,384]{1,0:T(8,128)S(1)} %copy-done.1, s32[1,6]{1,0:T(1,128)S(1)} %copy-done.2), custom_call_target="tpu_custom_call" | custom-call | tf_op jit(solution)/shard_map/merge/pallas_call | solution.py:413
  75.4 0.7 copy.5
Async XLA Ops:
  0.0 1.0 %copy-start = (f32[128,768]{1,0:T(8,128)S(1)}, f32[128,768]{1,0:T(8,128)}, u32[]{:S(2)}) copy-start(f32[128,768]{1,0:T(8,128)} %s_hbm.1) | copy-start | bytes 1179652
  1.0 0.9 %copy-start.1 = (f32[128,384]{1,0:T(8,128)S(1)}, f32[128,384]{1,0:T(8,128)}, u32[]{:S(2)}) copy-start(f32[128,384]{1,0:T(8,128)} %h_hbm.1) | copy-start | bytes 589828
  1.9 0.7 copy-start.2

commit v4 on v3

--- a/solution.py
+++ b/solution.py
@@ -241,7 +241,44 @@
         def nt(left, right):
             return dot3(left, right, True)
 
+        low_rows, mid_rows, top_rows = (low_own, low_other), (own, other), (top_own, top_other)
+
+        def load(ref, refs, *places):
+            for rows, columns in places:
+                high, low = split(ref[rows, columns])
+                refs[0][rows, columns] = high
+                refs[1][rows, columns] = low
+
+        def put(refs, rows, columns, value):
+            high, low = split(value)
+            refs[0][rows, columns] = high
+            refs[1][rows, columns] = low
+
+        def eye(n):
+            return (lax.broadcasted_iota(jnp.int32, (n, n), 0) == lax.broadcasted_iota(jnp.int32, (n, n), 1)).astype(F32)
+
+        def image_rows(h):
+            mid = split(z0[mid_rows[h], col(1, h)].T)
+            lower = split(z0[low_rows[h], col(1, h)].T)
+            upper = split(z0[top_rows[h], col(1, h)].T)
+            here = [pick(s_refs, mid_rows[h], cols(k)) for k in range(3)]
+            return [
+                split(nn(lower, pick(s_refs, low_rows[h], cols(0))) + nn(mid, here[0])),
+                split(nt(lower, pick(s_refs, row1, col(0, h))) + nn(mid, here[1]) + nt(upper, pick(s_refs, row1, col(2, h)))),
+                split(nn(mid, here[2]) + nn(upper, pick(s_refs, top_rows[h], cols(2)))),
+            ]
+
+        def half_cols(pair, h):
+            return pair[0][:, h * tile:(h + 1) * tile], pair[1][:, h * tile:(h + 1) * tile]
+
+        def diag_tiles(image, h, slot):
+            near_rows = (low_rows[h], mid_rows[h], top_rows[h])
+            return sum(nn(half_cols(image[f], h), pick(z_refs, near_rows[f], col(slot, h)))
+                       for f in range(3) if abs(f - slot) < 2)
+
         sn[other, col(1, 0)] = sn[own, col(1, 1)].T
+        load(sn, s_refs, (own, cols(0)), (own, cols(1)), (own, cols(2)), (other, col(1, 0)))
+        load(z0, z_refs, *[(own, cols(e)) for e in range(3)], *[(other, col(e, 0)) for e in range(3)])
         x_z[0].wait_recv()
         d_z0 = remote(z0.at[other, col(0, 1)], z0.at[top_other, col(1, 1)], "d")
         start([], [d_z0])
@@ -255,8 +292,6 @@
         u_s1 = remote(sx, spx_dn, "u")
         d_s1 = remote(sx, spx_up, "d")
         start([u_s1], [d_s1])
-        sn[other, col(1, 1)] = load_packed(sx, 0)
-        load_split(sn, s_refs, ((1, 1),))
 
         receive(u_own, d_own)
         sn[other, col(0, 0)] = so_dn[...].T
@@ -265,64 +300,107 @@
         sn[top_own, col(2, 0)] = load_packed(spo_up, 0)
         sn[low_other, col(0, 0)] = sn[low_own, col(0, 1)].T
         sn[top_other, col(2, 0)] = sn[top_own, col(2, 1)].T
-        load_split(sn, s_refs, ((1, 2),))
-        receive([u_z2], [d_z0])
-        load_split(z0, z_refs, ((0, 1), (2, 1), (1, 0), (1, 2)))
-        lower = split(z0[row0, cols(1)].T)
-        upper = split(z0[row2, cols(1)].T)
+        load(sn, s_refs, (low_own, cols(0)), (top_own, cols(2)), (other, col(0, 0)), (other, col(2, 0)),
+             (low_other, col(0, 0)), (top_other, col(2, 0)))
+        load(z0, z_refs, (low_own, cols(0)), (low_own, cols(1)), (top_own, cols(1)), (top_own, cols(2)),
+             (low_other, col(0, 0)), (low_other, col(1, 0)), (top_other, col(1, 0)), (top_other, col(2, 0)))
+        image_own = image_rows(0)
+        value = eye(tile) - diag_tiles(image_own, 0, 1)
+        store_packed(pd0, 0, value)
+        put(d_refs, own, col(1, 0), value)
+        for slot in (0, 2):
+            value = -diag_tiles(image_own, 0, slot)
+            d0[own, col(slot, 0)] = value
+            put(d_refs, own, col(slot, 0), value)
+        u_diag = [remote(pd0.at[pl.ds(0, 80)], qdn0.at[pl.ds(0, 80)], "u")]
+        d_diag = [remote(pd0.at[pl.ds(0, 80)], qup0.at[pl.ds(0, 80)], "d")]
+        u_edge = [remote(d0.at[own, col(2, 0)], d0.at[low_own, col(1, 0)], "u")]
+        d_edge = [remote(d0.at[own, col(0, 0)], d0.at[top_own, col(1, 0)], "d")]
+        sn[other, col(1, 1)] = load_packed(sx, 0)
+        load(sn, s_refs, (other, col(1, 1)), (other, col(2, 1)))
+        load(z0, z_refs, (other, col(0, 1)), (other, col(2, 1)))
 
         x_z[1].wait_recv()
         u_z1 = remote(z0.at[other, col(1, 1)], z0.at[low_other, col(0, 1)], "u")
         d_z1 = remote(z0.at[other, col(1, 1)], z0.at[top_other, col(2, 1)], "d")
-        start([u_z1], [d_z1])
-        load_split(z0, z_refs, ((1, 1),))
-        receive([u_s2, u_s1], [d_s1])
+        start([u_z1] + u_diag + u_edge, [d_z1] + d_diag + d_edge)
+        load(z0, z_refs, (other, col(1, 1)))
+        receive([u_z2, u_s2, u_s1], [d_z0, d_s1])
+        load(z0, z_refs, (low_other, col(1, 1)), (top_other, col(1, 1)))
         sn[other, col(0, 1)] = sx_dn[...].T
-        load_split(sn, s_refs, ((1, 0),))
         sn[low_other, col(0, 1)] = load_packed(spx_dn, 0)
         sn[top_other, col(2, 1)] = load_packed(spx_up, 0)
-        load_split(sn, s_refs, ((0, 0), (2, 2)))
-        ups, dns = [u_z1], [d_z1]
-
-        eye = (lax.broadcasted_iota(jnp.int32, (B, B), 0) == lax.broadcasted_iota(jnp.int32, (B, B), 1)).astype(F32)
+        load(sn, s_refs, (other, col(0, 1)), (low_other, col(0, 1)), (top_other, col(2, 1)))
+        image_other = image_rows(1)
+
+        def other_rows(slot):
+            return sum(nn(image_other[f], near(z_refs, f, slot)) for f in range(3) if abs(f - slot) < 2)
+
+        cross = -diag_tiles(image_own, 1, 1)
+        low_part = jnp.concatenate([jnp.zeros((tile, tile), F32), eye(tile)], axis=1) - other_rows(1)
+        pd0[pl.ds(80, tile), :] = cross
+        store_packed(pd0, 80 + tile, low_part[:, tile:])
+        rest = pl.ds(80, tile + 80)
+        u_diag.append(remote(pd0.at[rest], qdn0.at[rest], "u"))
+        d_diag.append(remote(pd0.at[rest], qup0.at[rest], "d"))
+        start(u_diag[1:], d_diag[1:])
+        put(d_refs, own, col(1, 1), cross)
+        put(d_refs, other, cols(1), low_part)
+        receive([u_z1], [d_z1])
+        load(z0, z_refs, (low_other, col(0, 1)), (top_other, col(2, 1)))
+        for slot in (2, 0):
+            cross = -diag_tiles(image_own, 1, slot)
+            low_part = -other_rows(slot)
+            d0[own, col(slot, 1)] = cross
+            d0[other, cols(slot)] = low_part
+            if slot == 2:
+                u_edge.append(remote(d0.at[own, col(2, 1)], d0.at[low_own, col(1, 1)], "u"))
+                u_edge.append(remote(d0.at[other, cols(2)], d0.at[low_other, cols(1)], "u"))
+                start(u_edge[1:], [])
+            else:
+                d_edge.append(remote(d0.at[own, col(0, 1)], d0.at[top_own, col(1, 1)], "d"))
+                d_edge.append(remote(d0.at[other, cols(0)], d0.at[top_other, cols(1)], "d"))
+                start([], d_edge[1:])
+            put(d_refs, own, col(slot, 1), cross)
+            put(d_refs, other, cols(slot), low_part)
 
         for step in range(ITERS):
             last = step == ITERS - 1
             z, d = (z0, d0) if step == 0 else (z1, d1)
             pd, q_dn, q_up = (pd0, qdn0, qup0) if step == 0 else (pd1, qdn1, qup1)
 
-            mid = split(z[row1, cols(1)].T)
-            t_own = [nn(mid, near(s_refs, 1, 0)), nt(mid, near(s_refs, 1, 1)), nn(mid, near(s_refs, 1, 2))]
             if step > 0:
+                mid = split(z[row1, cols(1)].T)
+                t_own = [nn(mid, near(s_refs, 1, 0)), nt(mid, near(s_refs, 1, 1)), nn(mid, near(s_refs, 1, 2))]
                 receive(*edge)
                 load_split(z, z_refs, ((0, 1), (2, 1)))
                 lower = split(z[row0, cols(1)].T)
                 upper = split(z[row2, cols(1)].T)
-            t = [
-                split(t_own[0] + nn(lower, near(s_refs, 0, 0))),
-                split(t_own[1] + nt(lower, near(s_refs, 1, 0)) + nt(upper, near(s_refs, 1, 2))),
-                split(t_own[2] + nn(upper, near(s_refs, 2, 2))),
-            ]
-            value = eye - (nn(t[0], near(z_refs, 0, 1)) + nn(t[1], near(z_refs, 1, 1)) + nn(t[2], near(z_refs, 2, 1)))
-            store_packed(pd, 0, value[:tile, :tile])
-            pd[pl.ds(80, tile), :] = value[:tile, tile:]
-            store_packed(pd, 80 + tile, value[tile:, tile:])
-            u_diag, d_diag = [remote(pd, q_dn, "u")], [remote(pd, q_up, "d")]
-            start(u_diag, d_diag)
-            keep_split(d_refs, 1, 1, value)
-
-            receive(ups, dns)
-            load_split(z, z_refs, ((0, 0), (2, 2)))
-            value = -(nn(t[1], near(z_refs, 1, 2)) + nn(t[2], near(z_refs, 2, 2)))
-            d[row1, cols(2)] = value
-            u_edge = remote(d.at[row1, cols(2)], d.at[row0, cols(1)], "u")
-            start([u_edge], [])
-            keep_split(d_refs, 1, 2, value)
-            value = -(nn(t[0], near(z_refs, 0, 0)) + nn(t[1], near(z_refs, 1, 0)))
-            d[row1, cols(0)] = value
-            d_edge = remote(d.at[row1, cols(0)], d.at[row2, cols(1)], "d")
-            start([], [d_edge])
-            keep_split(d_refs, 1, 0, value)
+                t = [
+                    split(t_own[0] + nn(lower, near(s_refs, 0, 0))),
+                    split(t_own[1] + nt(lower, near(s_refs, 1, 0)) + nt(upper, near(s_refs, 1, 2))),
+                    split(t_own[2] + nn(upper, near(s_refs, 2, 2))),
+                ]
+                value = eye(B) - (nn(t[0], near(z_refs, 0, 1)) + nn(t[1], near(z_refs, 1, 1)) + nn(t[2], near(z_refs, 2, 1)))
+                store_packed(pd, 0, value[:tile, :tile])
+                pd[pl.ds(80, tile), :] = value[:tile, tile:]
+                store_packed(pd, 80 + tile, value[tile:, tile:])
+                u_diag, d_diag = [remote(pd, q_dn, "u")], [remote(pd, q_up, "d")]
+                start(u_diag, d_diag)
+                keep_split(d_refs, 1, 1, value)
+
+                receive(ups, dns)
+                load_split(z, z_refs, ((0, 0), (2, 2)))
+                value = -(nn(t[1], near(z_refs, 1, 2)) + nn(t[2], near(z_refs, 2, 2)))
+                d[row1, cols(2)] = value
+                u_edge = [remote(d.at[row1, cols(2)], d.at[row0, cols(1)], "u")]
+                start(u_edge, [])
+                keep_split(d_refs, 1, 2, value)
+                value = -(nn(t[0], near(z_refs, 0, 0)) + nn(t[1], near(z_refs, 1, 0)))
+                d[row1, cols(0)] = value
+                d_edge = [remote(d.at[row1, cols(0)], d.at[row2, cols(1)], "d")]
+                start([], d_edge)
+                keep_split(d_refs, 1, 0, value)
 
             mine = own if last else row1
             left = [pick(z_refs, mine, cols(k)) for k in range(3)]
@@ -357,7 +435,7 @@
                         part = part * kx[r:r + 1, :]
                     z1[other, col(slot, g)] = part
 
-            receive([u_edge], [])
+            receive(u_edge, [])
             load_split(d, d_refs, ((0, 1),))
             first[0] = first[0] + nt(left[1], near(d_refs, 0, 1))
             f_low = split(first[0])
@@ -366,7 +444,7 @@
             if not last:
                 edge[1].append(remote(z1.at[row1, cols(0)], z1.at[row2, cols(1)], "d"))
                 start([], edge[1])
-            receive([], [d_edge])
+            receive([], d_edge)
             load_split(d, d_refs, ((2, 1),))
             first[2] = first[2] + nt(left[1], near(d_refs, 2, 1))
             f_high = split(first[2])

time: 76.3 us -> 75.4 us (0.988)
  Pallas kernels: 72.8 us -> 71.8 us
    pallas_call x1, Pallas kernels: 72.8 us -> 71.8 us  [per_device(): pl.pallas_call(make_kernel(n_blk, tile), out_shape=jax.ShapeDtypeStruct(i...]
where the time goes in v4:
time: 75.4 us; the launch traced here: 75.2 us
  Pallas kernels  71.8 us (95%)
  local copies, waits for them, and re-layouts  3.32 us (4%)
    pallas_call x1, Pallas kernels, per_device(): pl.pallas_call(make_kernel(n_blk, tile), out_shape=jax.ShapeDtypeStruct(i...  71.8 us
    unnamed x7, local copies, waits for them, and re-layouts  3.32 us

profile of v4, /device:TPU:1, one launch (start us, length us, event | category | flops | bytes accessed | tf_op | source)
XLA Modules:
  0.0 75.2 jit_solution(14223593532965312414)
XLA Ops:
  0.0 0.0 copy-start
  0.0 1.0 %copy-done = f32[128,768]{1,0:T(8,128)S(1)} copy-done((f32[128,768]{1,0:T(8,128)S(1)}, f32[128,768]{1,0:T(8,128)}, u32[]{:S(2)}) %copy-start) | copy-done | bytes 393240
  1.0 0.0 copy-start.1
  1.0 0.9 %copy-done.1 = f32[128,384]{1,0:T(8,128)S(1)} copy-done((f32[128,384]{1,0:T(8,128)S(1)}, f32[128,384]{1,0:T(8,128)}, u32[]{:S(2)}) %copy-start.1) | copy-done | bytes 196632
  1.9 0.0 copy-start.2
  1.9 0.7 copy-done.2
  2.6 71.8 %merge.1 = f32[128,768]{1,0:T(8,128)S(1)} custom-call(f32[128,768]{1,0:T(8,128)S(1)} %copy-done, f32[128,384]{1,0:T(8,128)S(1)} %copy-done.1, s32[1,6]{1,0:T(1,128)S(1)} %copy-done.2), custom_call_target="tpu_custom_call" | custom-call | tf_op jit(solution)/shard_map/merge/pallas_call | solution.py:491
  74.4 0.7 copy.5
Async XLA Ops:
  0.0 1.0 %copy-start = (f32[128,768]{1,0:T(8,128)S(1)}, f32[128,768]{1,0:T(8,128)}, u32[]{:S(2)}) copy-start(f32[128,768]{1,0:T(8,128)} %s_hbm.1) | copy-start | bytes 1179652
  1.0 0.9 %copy-start.1 = (f32[128,384]{1,0:T(8,128)S(1)}, f32[128,384]{1,0:T(8,128)}, u32[]{:S(2)}) copy-start(f32[128,384]{1,0:T(8,128)} %h_hbm.1) | copy-start | bytes 589828
  1.9 0.7 copy-start.2

commit v5 on v4

--- a/solution.py
+++ b/solution.py
@@ -346,23 +346,27 @@
         start(u_diag[1:], d_diag[1:])
         put(d_refs, own, col(1, 1), cross)
         put(d_refs, other, cols(1), low_part)
+        part = {}
+        for slot in (2, 0):
+            part[slot] = (nn(half_cols(image_own[1], 1), pick(z_refs, other, col(slot, 1))),
+                          nn(image_other[1], near(z_refs, 1, slot)))
         receive([u_z1], [d_z1])
         load(z0, z_refs, (low_other, col(0, 1)), (top_other, col(2, 1)))
-        for slot in (2, 0):
-            cross = -diag_tiles(image_own, 1, slot)
-            low_part = -other_rows(slot)
+        edges = {}
+        for slot, rows in ((2, top_other), (0, low_other)):
+            cross = -(part[slot][0] + nn(half_cols(image_own[slot], 1), pick(z_refs, rows, col(slot, 1))))
+            low_part = -(part[slot][1] + nn(image_other[slot], near(z_refs, slot, slot)))
             d0[own, col(slot, 1)] = cross
             d0[other, cols(slot)] = low_part
-            if slot == 2:
-                u_edge.append(remote(d0.at[own, col(2, 1)], d0.at[low_own, col(1, 1)], "u"))
-                u_edge.append(remote(d0.at[other, cols(2)], d0.at[low_other, cols(1)], "u"))
-                start(u_edge[1:], [])
-            else:
-                d_edge.append(remote(d0.at[own, col(0, 1)], d0.at[top_own, col(1, 1)], "d"))
-                d_edge.append(remote(d0.at[other, cols(0)], d0.at[top_other, cols(1)], "d"))
-                start([], d_edge[1:])
-            put(d_refs, own, col(slot, 1), cross)
-            put(d_refs, other, cols(slot), low_part)
+            edges[slot] = cross, low_part
+        u_edge.append(remote(d0.at[own, col(2, 1)], d0.at[low_own, col(1, 1)], "u"))
+        u_edge.append(remote(d0.at[other, cols(2)], d0.at[low_other, cols(1)], "u"))
+        d_edge.append(remote(d0.at[own, col(0, 1)], d0.at[top_own, col(1, 1)], "d"))
+        d_edge.append(remote(d0.at[other, cols(0)], d0.at[top_other, cols(1)], "d"))
+        start(u_edge[1:], d_edge[1:])
+        for slot in (2, 0):
+            put(d_refs, own, col(slot, 1), edges[slot][0])
+            put(d_refs, other, cols(slot), edges[slot][1])
 
         for step in range(ITERS):
             last = step == ITERS - 1
@@ -389,18 +393,18 @@
                 start(u_diag, d_diag)
                 keep_split(d_refs, 1, 1, value)
 
+                part_up, part_dn = nn(t[1], near(z_refs, 1, 2)), nn(t[1], near(z_refs, 1, 0))
                 receive(ups, dns)
                 load_split(z, z_refs, ((0, 0), (2, 2)))
-                value = -(nn(t[1], near(z_refs, 1, 2)) + nn(t[2], near(z_refs, 2, 2)))
-                d[row1, cols(2)] = value
+                value_up = -(part_up + nn(t[2], near(z_refs, 2, 2)))
+                value_dn = -(part_dn + nn(t[0], near(z_refs, 0, 0)))
+                d[row1, cols(2)] = value_up
+                d[row1, cols(0)] = value_dn
                 u_edge = [remote(d.at[row1, cols(2)], d.at[row0, cols(1)], "u")]
-                start(u_edge, [])
-                keep_split(d_refs, 1, 2, value)
-                value = -(nn(t[0], near(z_refs, 0, 0)) + nn(t[1], near(z_refs, 1, 0)))
-                d[row1, cols(0)] = value
                 d_edge = [remote(d.at[row1, cols(0)], d.at[row2, cols(1)], "d")]
-                start([], d_edge)
-                keep_split(d_refs, 1, 0, value)
+                start(u_edge, d_edge)
+                keep_split(d_refs, 1, 2, value_up)
+                keep_split(d_refs, 1, 0, value_dn)
 
             mine = own if last else row1
             left = [pick(z_refs, mine, cols(k)) for k in range(3)]
@@ -435,23 +439,18 @@
                         part = part * kx[r:r + 1, :]
                     z1[other, col(slot, g)] = part
 
-            receive(u_edge, [])
-            load_split(d, d_refs, ((0, 1),))
+            receive(u_edge, d_edge)
+            load_split(d, d_refs, ((0, 1), (2, 1)))
             first[0] = first[0] + nt(left[1], near(d_refs, 0, 1))
-            f_low = split(first[0])
+            first[2] = first[2] + nt(left[1], near(d_refs, 2, 1))
+            f_low, f_high = split(first[0]), split(first[2])
             finish(0, nt(f_low, near(d_refs, 0, 0)) + nt(f_mid, near(d_refs, 0, 1)))
+            finish(2, nt(f_high, near(d_refs, 2, 2)) + nt(f_mid, near(d_refs, 2, 1)))
             edge = [[], []]
             if not last:
+                edge[0].append(remote(z1.at[row1, cols(2)], z1.at[row0, cols(1)], "u"))
                 edge[1].append(remote(z1.at[row1, cols(0)], z1.at[row2, cols(1)], "d"))
-                start([], edge[1])
-            receive([], d_edge)
-            load_split(d, d_refs, ((2, 1),))
-            first[2] = first[2] + nt(left[1], near(d_refs, 2, 1))
-            f_high = split(first[2])
-            finish(2, nt(f_mid, near(d_refs, 2, 1)) + nt(f_high, near(d_refs, 2, 2)))
-            if not last:
-                edge[0].append(remote(z1.at[row1, cols(2)], z1.at[row0, cols(1)], "u"))
-                start(edge[0], [])
+                start(*edge)
             finish(1, second_mid + nt(f_low, near(d_refs, 1, 0)) + nt(f_high, near(d_refs, 1, 2)))
             if not last:
                 ups = [remote(z1.at[row1, cols(1)], z1.at[row0, cols(0)], "u")]

time: 75.4 us -> 74.7 us (level)
  no operation moved by 1% of the time
where the time goes in v5:
time: 74.7 us; the launch traced here: 74.6 us
  Pallas kernels  71.2 us (95%)
  local copies, waits for them, and re-layouts  3.32 us (4%)
    pallas_call x1, Pallas kernels, per_device(): pl.pallas_call(make_kernel(n_blk, tile), out_shape=jax.ShapeDtypeStruct(i...  71.2 us
    unnamed x7, local copies, waits for them, and re-layouts  3.32 us

profile of v5, /device:TPU:1, one launch (start us, length us, event | category | flops | bytes accessed | tf_op | source)
XLA Modules:
  0.0 74.6 jit_solution(12046356059031016746)
XLA Ops:
  0.0 0.0 copy-start
  0.0 1.0 %copy-done = f32[128,768]{1,0:T(8,128)S(1)} copy-done((f32[128,768]{1,0:T(8,128)S(1)}, f32[128,768]{1,0:T(8,128)}, u32[]{:S(2)}) %copy-start) | copy-done | bytes 393240
  1.0 0.0 copy-start.1
  1.0 0.9 %copy-done.1 = f32[128,384]{1,0:T(8,128)S(1)} copy-done((f32[128,384]{1,0:T(8,128)S(1)}, f32[128,384]{1,0:T(8,128)}, u32[]{:S(2)}) %copy-start.1) | copy-done | bytes 196632
  1.9 0.0 copy-start.2
  1.9 0.7 copy-done.2
  2.6 71.2 %merge.1 = f32[128,768]{1,0:T(8,128)S(1)} custom-call(f32[128,768]{1,0:T(8,128)S(1)} %copy-done, f32[128,384]{1,0:T(8,128)S(1)} %copy-done.1, s32[1,6]{1,0:T(1,128)S(1)} %copy-done.2), custom_call_target="tpu_custom_call" | custom-call | tf_op jit(solution)/shard_map/merge/pallas_call | solution.py:490
  73.8 0.7 %copy.5 = f32[128,768]{1,0:T(8,128)} copy(f32[128,768]{1,0:T(8,128)S(1)} %merge.1) | data formatting | bytes 786432
Async XLA Ops:
  0.0 1.0 %copy-start = (f32[128,768]{1,0:T(8,128)S(1)}, f32[128,768]{1,0:T(8,128)}, u32[]{:S(2)}) copy-start(f32[128,768]{1,0:T(8,128)} %s_hbm.1) | copy-start | bytes 1179652
  1.0 0.9 %copy-start.1 = (f32[128,384]{1,0:T(8,128)S(1)}, f32[128,384]{1,0:T(8,128)}, u32[]{:S(2)}) copy-start(f32[128,384]{1,0:T(8,128)} %h_hbm.1) | copy-start | bytes 589828
  1.9 0.7 copy-start.2

commit v6 on v5

--- a/solution.py
+++ b/solution.py
@@ -149,11 +149,9 @@
         x_s1 = remote(sp, sx, "x")
         x_s2 = remote(sn.at[own, col(2, 0)], sn.at[other, col(2, 1)], "x")
         x_k = remote(kbuf, kx, "x")
+        store_packed(sp, 0, sn[own, col(1, 0)])
         for c in (x_z[0], x_z[2], x_s2):
             c.start()
-        store_packed(sp, 0, sn[own, col(1, 0)])
-        x_s1.start()
-        x_z[1].start()
 
         u_own = [
             remote(z0.at[own, col(2, 0)], z0.at[low_own, col(1, 0)], "u"),
@@ -170,6 +168,8 @@
             remote(z0.at[own, col(1, 0)], z0.at[top_own, col(2, 0)], "d"),
         ]
         start(u_own, d_own)
+        for c in (x_s1, x_z[1]):
+            c.start()
 
         zp_load.wait()
         keep_own = [zp_ref[0, 2 * e + half_of(g)].astype(F32) for e in range(3) for g in range(2)]

time: 74.7 us -> 73.8 us (0.988)
  Pallas kernels: 71.2 us -> 70.3 us
    pallas_call x1, Pallas kernels: 71.2 us -> 70.3 us  [per_device(): pl.pallas_call(make_kernel(n_blk, tile), out_shape=jax.ShapeDtypeStruct(i...]
where the time goes in v6:
time: 73.8 us; the launch traced here: 73.6 us
  Pallas kernels  70.3 us (95%)
  local copies, waits for them, and re-layouts  3.32 us (4%)
    pallas_call x1, Pallas kernels, per_device(): pl.pallas_call(make_kernel(n_blk, tile), out_shape=jax.ShapeDtypeStruct(i...  70.3 us
    unnamed x7, local copies, waits for them, and re-layouts  3.32 us

profile of v6, /device:TPU:1, one launch (start us, length us, event | category | flops | bytes accessed | tf_op | source)
XLA Modules:
  0.0 73.6 jit_solution(3493566620841977975)
XLA Ops:
  0.0 0.0 copy-start
  0.0 1.0 %copy-done = f32[128,768]{1,0:T(8,128)S(1)} copy-done((f32[128,768]{1,0:T(8,128)S(1)}, f32[128,768]{1,0:T(8,128)}, u32[]{:S(2)}) %copy-start) | copy-done | bytes 393240
  1.0 0.0 copy-start.1
  1.0 0.9 %copy-done.1 = f32[128,384]{1,0:T(8,128)S(1)} copy-done((f32[128,384]{1,0:T(8,128)S(1)}, f32[128,384]{1,0:T(8,128)}, u32[]{:S(2)}) %copy-start.1) | copy-done | bytes 196632
  1.9 0.0 copy-start.2
  1.9 0.7 copy-done.2
  2.6 70.3 %merge.1 = f32[128,768]{1,0:T(8,128)S(1)} custom-call(f32[128,768]{1,0:T(8,128)S(1)} %copy-done, f32[128,384]{1,0:T(8,128)S(1)} %copy-done.1, s32[1,6]{1,0:T(1,128)S(1)} %copy-done.2), custom_call_target="tpu_custom_call" | custom-call | tf_op jit(solution)/shard_map/merge/pallas_call | solution.py:490
  72.8 0.7 %copy.5 = f32[128,768]{1,0:T(8,128)} copy(f32[128,768]{1,0:T(8,128)S(1)} %merge.1) | data formatting | bytes 786432
Async XLA Ops:
  0.0 1.0 %copy-start = (f32[128,768]{1,0:T(8,128)S(1)}, f32[128,768]{1,0:T(8,128)}, u32[]{:S(2)}) copy-start(f32[128,768]{1,0:T(8,128)} %s_hbm.1) | copy-start | bytes 1179652
  1.0 0.9 %copy-start.1 = (f32[128,384]{1,0:T(8,128)S(1)}, f32[128,384]{1,0:T(8,128)}, u32[]{:S(2)}) copy-start(f32[128,384]{1,0:T(8,128)} %h_hbm.1) | copy-start | bytes 589828
  1.9 0.7 copy-start.2

commit v7 on v6

--- a/solution.py
+++ b/solution.py
@@ -316,6 +316,7 @@
         d_diag = [remote(pd0.at[pl.ds(0, 80)], qup0.at[pl.ds(0, 80)], "d")]
         u_edge = [remote(d0.at[own, col(2, 0)], d0.at[low_own, col(1, 0)], "u")]
         d_edge = [remote(d0.at[own, col(0, 0)], d0.at[top_own, col(1, 0)], "d")]
+        start(u_diag + u_edge, d_diag + d_edge)
         sn[other, col(1, 1)] = load_packed(sx, 0)
         load(sn, s_refs, (other, col(1, 1)), (other, col(2, 1)))
         load(z0, z_refs, (other, col(0, 1)), (other, col(2, 1)))
@@ -323,7 +324,7 @@
         x_z[1].wait_recv()
         u_z1 = remote(z0.at[other, col(1, 1)], z0.at[low_other, col(0, 1)], "u")
         d_z1 = remote(z0.at[other, col(1, 1)], z0.at[top_other, col(2, 1)], "d")
-        start([u_z1] + u_diag + u_edge, [d_z1] + d_diag + d_edge)
+        start([u_z1], [d_z1])
         load(z0, z_refs, (other, col(1, 1)))
         receive([u_z2, u_s2, u_s1], [d_z0, d_s1])
         load(z0, z_refs, (low_other, col(1, 1)), (top_other, col(1, 1)))
@@ -418,8 +419,8 @@
                 top = jnp.concatenate([load_packed(ref, 0), cross], axis=1)
                 low = jnp.concatenate([cross.T, load_packed(ref, 80 + tile)], axis=1)
                 keep_split(d_refs, row, row, jnp.concatenate([top, low], axis=0))
-            first[0] = nt(left[0], near(d_refs, 0, 0))
-            first[2] = nt(left[2], near(d_refs, 2, 2))
+            first[0] = nn(left[0], near(d_refs, 0, 0))
+            first[2] = nn(left[2], near(d_refs, 2, 2))
             if step == 0:
                 x_k.wait_recv()
 
@@ -444,8 +445,8 @@
             first[0] = first[0] + nt(left[1], near(d_refs, 0, 1))
             first[2] = first[2] + nt(left[1], near(d_refs, 2, 1))
             f_low, f_high = split(first[0]), split(first[2])
-            finish(0, nt(f_low, near(d_refs, 0, 0)) + nt(f_mid, near(d_refs, 0, 1)))
-            finish(2, nt(f_high, near(d_refs, 2, 2)) + nt(f_mid, near(d_refs, 2, 1)))
+            finish(0, nn(f_low, near(d_refs, 0, 0)) + nt(f_mid, near(d_refs, 0, 1)))
+            finish(2, nn(f_high, near(d_refs, 2, 2)) + nt(f_mid, near(d_refs, 2, 1)))
             edge = [[], []]
             if not last:
                 edge[0].append(remote(z1.at[row1, cols(2)], z1.at[row0, cols(1)], "u"))

time: 73.8 us -> 74.2 us (level)
  no operation moved by 1% of the time
where the time goes in v7:
time: 74.2 us; the launch traced here: 74 us
  Pallas kernels  70.7 us (95%)
  local copies, waits for them, and re-layouts  3.32 us (4%)
    pallas_call x1, Pallas kernels, per_device(): pl.pallas_call(make_kernel(n_blk, tile), out_shape=jax.ShapeDtypeStruct(i...  70.7 us
    unnamed x7, local copies, waits for them, and re-layouts  3.32 us

profile of v7, /device:TPU:1, one launch (start us, length us, event | category | flops | bytes accessed | tf_op | source)
XLA Modules:
  0.0 74.0 jit_solution(14193758287424905554)
XLA Ops:
  0.0 0.0 copy-start
  0.0 1.0 %copy-done = f32[128,768]{1,0:T(8,128)S(1)} copy-done((f32[128,768]{1,0:T(8,128)S(1)}, f32[128,768]{1,0:T(8,128)}, u32[]{:S(2)}) %copy-start) | copy-done | bytes 393240
  1.0 0.0 copy-start.1
  1.0 0.9 %copy-done.1 = f32[128,384]{1,0:T(8,128)S(1)} copy-done((f32[128,384]{1,0:T(8,128)S(1)}, f32[128,384]{1,0:T(8,128)}, u32[]{:S(2)}) %copy-start.1) | copy-done | bytes 196632
  1.9 0.0 copy-start.2
  1.9 0.7 copy-done.2
  2.6 70.7 %merge.1 = f32[128,768]{1,0:T(8,128)S(1)} custom-call(f32[128,768]{1,0:T(8,128)S(1)} %copy-done, f32[128,384]{1,0:T(8,128)S(1)} %copy-done.1, s32[1,6]{1,0:T(1,128)S(1)} %copy-done.2), custom_call_target="tpu_custom_call" | custom-call | tf_op jit(solution)/shard_map/merge/pallas_call | solution.py:491
  73.2 0.7 %copy.5 = f32[128,768]{1,0:T(8,128)} copy(f32[128,768]{1,0:T(8,128)S(1)} %merge.1) | data formatting | bytes 786432
Async XLA Ops:
  0.0 1.0 %copy-start = (f32[128,768]{1,0:T(8,128)S(1)}, f32[128,768]{1,0:T(8,128)}, u32[]{:S(2)}) copy-start(f32[128,768]{1,0:T(8,128)} %s_hbm.1) | copy-start | bytes 1179652
  1.0 0.9 %copy-start.1 = (f32[128,384]{1,0:T(8,128)S(1)}, f32[128,384]{1,0:T(8,128)}, u32[]{:S(2)}) copy-start(f32[128,384]{1,0:T(8,128)} %h_hbm.1) | copy-start | bytes 589828
  1.9 0.7 copy-start.2
